TPU v7x, 32 devices: a 4x4x1 block of a 4x4x8 slice. The times are simulated.
32 devices in a mesh: dp: 1 (over z), sp: 32 (over y, x, core).
Axes of the slice: x: 4, y: 4, z: 1, core: 2. Of those that a mesh axis runs over, the one named last changes fastest.
The devices are a block of a 4x4x8 slice.
Arguments:
- patches: bfloat16 [16, 16384, 768], P('dp', 'sp')
- ln1_scale: float32 [768], replicated
- ln1_bias: float32 [768], replicated
- w_tok1: bfloat16 [16384, 384], replicated
- b_tok1: float32 [384], replicated
- w_tok2: bfloat16 [384, 16384], replicated
- b_tok2: float32 [16384], replicated
- ln2_scale: float32 [768], replicated
- ln2_bias: float32 [768], replicated
- w_ch1: bfloat16 [768, 3072], replicated
- b_ch1: float32 [3072], replicated
- w_ch2: bfloat16 [3072, 768], replicated
- b_ch2: float32 [768], replicated
Outputs:
- output: bfloat16 [16, 16384, 768], P('dp', 'sp')
All inputs are finite; a program needn't handle non-finite values.
Results may differ from a plain program's by a relative error of at most 0.0112.
Values are sent between devices in bfloat16 or wider.
A program may use at most 768 MiB of HBM per device.

v0:
```python
import jax
import jax.numpy as jnp
from jax import lax
from jax.sharding import PartitionSpec as P

LN_EPS = 1e-6


def layer_norm(rows, scale, offset):
    rows_wide = rows.astype(jnp.float32)
    row_mean = jnp.mean(rows_wide, axis=-1, keepdims=True)
    centered = rows_wide - row_mean
    row_var = jnp.mean(centered * centered, axis=-1, keepdims=True)
    return (centered * lax.rsqrt(row_var + LN_EPS) * scale + offset).astype(jnp.bfloat16)


def channel_mixing(residual, ln2_scale, ln2_bias, w_ch1, b_ch1, w_ch2, b_ch2):
    chan_in = layer_norm(residual, ln2_scale, ln2_bias)
    pre_act = jnp.einsum('bsc,ce->bse', chan_in, w_ch1, preferred_element_type=jnp.float32) + b_ch1
    act_ch = jax.nn.gelu(pre_act, approximate=True).astype(jnp.bfloat16)
    ch_out = jnp.einsum('bse,ec->bsc', act_ch, w_ch2, preferred_element_type=jnp.float32) + b_ch2
    return (residual.astype(jnp.float32) + ch_out).astype(jnp.bfloat16)


def solution(mesh):
    row_spec = P('dp', 'sp', None)
    full_spec = P()

    def local_layer(patches, ln1_scale, ln1_bias, w_tok1, b_tok1, w_tok2, b_tok2, ln2_scale, ln2_bias, w_ch1, b_ch1, w_ch2, b_ch2):
        normed = layer_norm(patches, ln1_scale, ln1_bias)
        normed_cols = lax.all_to_all(normed, 'sp', 2, 1, tiled=True)
        hidden = jnp.einsum('sd,bsc->bdc', w_tok1, normed_cols, preferred_element_type=jnp.float32)
        act_tok = jax.nn.gelu(hidden + b_tok1[None, :, None], approximate=True).astype(jnp.bfloat16)
        mixed = jnp.einsum('ds,bdc->bsc', w_tok2, act_tok, preferred_element_type=jnp.float32)
        mixed_cols = (mixed + b_tok2[None, :, None]).astype(jnp.bfloat16)
        mixed_rows = lax.all_to_all(mixed_cols, 'sp', 1, 2, tiled=True)
        residual = (patches.astype(jnp.float32) + mixed_rows.astype(jnp.float32)).astype(jnp.bfloat16)
        return channel_mixing(residual, ln2_scale, ln2_bias, w_ch1, b_ch1, w_ch2, b_ch2)

    return jax.shard_map(local_layer, mesh=mesh, in_specs=(row_spec,) + (full_spec,) * 12, out_specs=row_spec, check_vma=False)
```

profile of v0, /device:TPU:96, one launch (start us, length us, event | category | flops | bytes accessed | tf_op | source)
XLA Modules:
  0.0 951.6 jit_solution(3242401909119185889)
XLA Ops:
  0.0 0.0 copy-start
  0.0 0.0 copy-start.1
  0.0 6.3 convert_reduce_fusion.1
  6.3 8.2 fusion.18
  14.6 0.0 copy-done
  14.6 0.0 copy-done.1
  14.6 12.5 %fusion.21 = bf16[16,512,768]{2,1,0:T(8,128)(2,1)} fusion(bf16[16,512,768]{2,1,0:T(8,128)(2,1)} %param.13, f32[768]{0:T(1024)S(1)} %copy-done, f32[768]{0:T(1024)S(1)} %copy-done.1, f32[16,512]{1,0:T(8,128)S(1)} %add_rsqrt_fusion.1, f32[16,512]{1,0:T(8,128)S(1)} %broadcast_multiply_fusion.1), kind=kLoop, calls=%fused_computation.27 | loop fusion | flops 37748736 | bytes 25237504 | tf_op jit(solution)/shard_map/convert_element_type | solution.py:14
  27.1 17.0 %copy.32 = bf16[16,512,768]{1,0,2:T(8,128)(2,1)} copy(bf16[16,512,768]{2,1,0:T(8,128)(2,1)} %fusion.21) | data formatting | bytes 25165824 | tf_op jit(solution)/shard_map/convert_element_type | solution.py:14
  44.0 165.6 %all_to_all.27 = bf16[16,512,768]{1,0,2:T(8,128)(2,1)S(1)} all-to-all(bf16[16,512,768]{1,0,2:T(8,128)(2,1)} %copy.32), channel_id=1, replica_groups=mesh['dp'=1,'sp'=32] {'sp'}, dimensions={2} | all-to-all | bytes 25165824 | tf_op jit(solution)/shard_map/all_to_all | solution.py:31
  209.7 0.0 copy-start.7
  209.7 19.3 %copy.34 = bf16[16,32,512,24]{2,1,3,0:T(8,128)(2,1)} copy(bf16[16,32,512,24]{2,0,3,1:T(8,128)(2,1)S(1)} %bitcast.57) | data formatting | bytes 25165824 | tf_op jit(solution)/shard_map/all_to_all | solution.py:31
  229.0 19.6 %all_to_all.23 = bf16[16,16384,24]{1,2,0:T(8,128)(2,1)} reshape(bf16[16,32,512,24]{2,1,3,0:T(8,128)(2,1)} %copy.34) | data formatting | bytes 25165824 | tf_op jit(solution)/shard_map/all_to_all | solution.py:31
  248.5 0.0 copy-done.7
  248.5 0.0 copy-start.2
  248.5 13.5 %fusion.64 = bf16[16,384,24]{1,2,0:T(8,128)(2,1)S(1)} fusion(bf16[16,16384,24]{1,2,0:T(8,128)(2,1)} %all_to_all.23, bf16[16384,384]{1,0:T(8,128)(2,1)} %param.16, f32[384]{0:T(512)S(1)} %copy-done.7), kind=kOutput, calls=%fused_computation.52 | convolution fusion | flops 4833312768 | bytes 25462272 | tf_op jit(solution)/shard_map/sd,bsc->bdc/dot_general | solution.py:32
  262.0 0.0 copy-done.2
  262.0 14.2 %fusion.24 = bf16[16,16384,24]{1,2,0:T(8,128)(2,1)} fusion(bf16[16,384,24]{1,2,0:T(8,128)(2,1)S(1)} %fusion.64, bf16[384,16384]{1,0:T(8,128)(2,1)} %param.18, f32[16384]{0:T(1024)S(1)} %copy-done.2), kind=kOutput, calls=%fused_computation.31 | convolution fusion | flops 4844421120 | bytes 25526272 | tf_op jit(solution)/shard_map/ds,bdc->bsc/dot_general | solution.py:34
  276.2 56.0 %copy.35 = bf16[16,16384,24]{2,0,1:T(8,128)(2,1)} copy(bf16[16,16384,24]{1,2,0:T(8,128)(2,1)} %fusion.24) | data formatting | bytes 25165824 | tf_op jit(solution)/shard_map/convert_element_type | solution.py:35
  332.2 90.6 %reshape.42 = bf16[32,2,98304]{2,1,0:T(2,128)(2,1)} reshape(bf16[16384,16,24]{2,1,0:T(8,128)(2,1)} %bitcast.45) | data formatting | bytes 25165824
  422.8 155.9 %all_to_all.28 = bf16[32,2,98304]{2,1,0:T(2,128)(2,1)} all-to-all(bf16[32,2,98304]{2,1,0:T(2,128)(2,1)} %reshape.42), channel_id=1, replica_groups=mesh['dp'=1,'sp'=32] {'sp'}, dimensions={0} | all-to-all | bytes 25165824 | tf_op jit(solution)/shard_map/all_to_all | solution.py:36
  578.8 96.0 %reshape.43 = bf16[16384,16,24]{2,1,0:T(8,128)(2,1)} reshape(bf16[32,2,98304]{2,1,0:T(2,128)(2,1)} %all_to_all.28) | data formatting | bytes 25165824
  674.7 58.0 %copy.36 = bf16[16,16384,24]{1,2,0:T(8,128)(2,1)} copy(bf16[16,16384,24]{2,0,1:T(8,128)(2,1)} %bitcast.46) | data formatting | bytes 25165824 | tf_op jit(solution)/shard_map/all_to_all | solution.py:36
  732.7 6.5 convert_element_type.60
  739.3 20.0 %copy.40 = f32[48,8,32,512]{3,2,1,0:T(8,128)} copy(f32[48,8,32,512]{3,1,2,0:T(8,128)S(1)} %bitcast.54) | data formatting | bytes 50331648
  759.2 27.1 %copy.37 = f32[16,512,32,24]{1,3,2,0:T(8,128)} copy(f32[16,512,32,24]{1,2,3,0:T(8,128)} %bitcast.55) | data formatting | bytes 50331648 | tf_op jit(solution)/shard_map/convert_element_type | solution.py:37
  786.3 24.7 %copy.38 = f32[16,512,768]{2,1,0:T(8,128)} copy(f32[16,512,768]{1,2,0:T(8,128)} %bitcast.56) | data formatting | bytes 50331648 | tf_op jit(solution)/shard_map/convert_element_type | solution.py:37
  811.0 0.0 copy-start.3
  811.0 0.0 copy-start.4
  811.0 0.0 copy-start.5
  811.0 17.6 %convert_reduce_fusion = (f32[16,512]{1,0:T(8,128)S(1)}, bf16[16,512,768]{2,1,0:T(8,128)(2,1)}) fusion(f32[16,512,768]{2,1,0:T(8,128)} %copy.38, bf16[16,512,768]{2,1,0:T(8,128)(2,1)} %param.13), kind=kLoop, calls=%fused_computation.12 | loop fusion | flops 31449088 | bytes 50364416 | tf_op jit(solution)/shard_map/reduce_sum | solution.py:11
  828.6 8.2 fusion.14
  836.9 0.0 copy-done.3
  836.9 0.0 copy-done.4
  836.9 0.0 copy-done.5
  836.9 0.0 copy-start.6
  836.9 65.1 %fusion.83 = bf16[16,512,3072]{2,1,0:T(8,128)(2,1)} fusion(f32[3072]{0:T(1024)S(1)} %copy-done.3, bf16[16,512,768]{2,1,0:T(8,128)(2,1)} %get-tuple-element.6, f32[768]{0:T(1024)S(1)} %copy-done.4, f32[768]{0:T(1024)S(1)} %copy-done.5, f32[16,512]{1,0:T(8,128)S(1)} %add_rsqrt_fusion, f32[16,512]{1,0:T(8,128)S(1)} %broadcast_multiply_fusion, ...), kind=kOutput, calls=%fused_computation.8.clone.clone.clone.clone.1 | convolution fusion | flops 38944112640 | bytes 67717120 | tf_op jit(solution)/shard_map/bsc,ce->bse/dot_general | solution.py:19
  902.0 0.0 copy-done.6
  902.0 49.2 %fusion.23 = bf16[16,512,768]{2,1,0:T(8,128)(2,1)} fusion(bf16[16,512,768]{2,1,0:T(8,128)(2,1)} %get-tuple-element.6, f32[768]{0:T(1024)S(1)} %copy-done.6, bf16[3072,768]{1,0:T(8,128)(2,1)} %param.24, bf16[16,512,3072]{2,1,0:T(8,128)(2,1)} %fusion.83), kind=kOutput, calls=%fused_computation.29 | convolution fusion | flops 38679871488 | bytes 80219136 | tf_op jit(solution)/shard_map/bse,ec->bsc/dot_general | solution.py:21
  (4 shorter events, 0.0 us)
Async XLA Ops:
  0.0 14.6 %copy-start = (f32[768]{0:T(1024)S(1)}, f32[768]{0:T(1024)}, u32[]{:S(2)}) copy-start(f32[768]{0:T(1024)} %param.15) | copy-start | bytes 9220
  0.0 14.6 %copy-start.1 = (f32[768]{0:T(1024)S(1)}, f32[768]{0:T(1024)}, u32[]{:S(2)}) copy-start(f32[768]{0:T(1024)} %param.14) | copy-start | bytes 9220
  209.7 38.8 %copy-start.7 = (f32[384]{0:T(512)S(1)}, f32[384]{0:T(512)}, u32[]{:S(2)}) copy-start(f32[384]{0:T(512)} %param.17) | copy-start | bytes 4612
  248.5 13.5 %copy-start.2 = (f32[16384]{0:T(1024)S(1)}, f32[16384]{0:T(1024)}, u32[]{:S(2)}) copy-start(f32[16384]{0:T(1024)} %param.19) | copy-start | bytes 196612
  811.0 25.9 %copy-start.3 = (f32[3072]{0:T(1024)S(1)}, f32[3072]{0:T(1024)}, u32[]{:S(2)}) copy-start(f32[3072]{0:T(1024)} %param.23) | copy-start | bytes 36868
  811.0 25.9 %copy-start.4 = (f32[768]{0:T(1024)S(1)}, f32[768]{0:T(1024)}, u32[]{:S(2)}) copy-start(f32[768]{0:T(1024)} %param.21) | copy-start | bytes 9220
  811.0 25.9 %copy-start.5 = (f32[768]{0:T(1024)S(1)}, f32[768]{0:T(1024)}, u32[]{:S(2)}) copy-start(f32[768]{0:T(1024)} %param.20) | copy-start | bytes 9220
  836.9 65.1 %copy-start.6 = (f32[768]{0:T(1024)S(1)}, f32[768]{0:T(1024)}, u32[]{:S(2)}) copy-start(f32[768]{0:T(1024)} %param.25) | copy-start | bytes 9220
where the time goes:
time: 965 us; the launch traced here: 952 us
  local copies, waits for them, and re-layouts  428 us (44%)
  blocking collectives  322 us (33%)
  matrix products  142 us (15%)
  other arithmetic  59.4 us (6%)
    unnamed x19, local copies, waits for them, and re-layouts  207 us
    all_to_all x1, blocking collectives, local_layer(): normed_cols = lax.all_to_all(normed, 'sp', 2, 1, tiled=True)  166 us
    all_to_all x1, blocking collectives, local_layer(): mixed_rows = lax.all_to_all(mixed_cols, 'sp', 1, 2, tiled=True)  156 us
    dot_general x1, matrix products, channel_mixing(): jnp.einsum('bsc,ce->bse', chan_in, w_ch1, preferred_element_type=jnp.floa...  65.1 us
    all_to_all x1, local copies, waits for them, and re-layouts, local_layer(): mixed_rows = lax.all_to_all(mixed_cols, 'sp', 1, 2, tiled=True)  58 us
    convert_element_type x1, local copies, waits for them, and re-layouts, local_layer(): mixed_cols = (mixed + b_tok2[None, :, None]).astype(jnp.bfloat16)  56 us
    convert_element_type x2, local copies, waits for them, and re-layouts, local_layer(): mixed_rows.astype(jnp.float32)  51.7 us
    dot_general x1, matrix products, channel_mixing(): jnp.einsum('bse,ec->bsc', act_ch, w_ch2, preferred_element_type=jnp.float32)  49.2 us

commit v1 on v0

v1 whole, which is shorter than its diff:
```python
import functools
import math

import jax
import jax.numpy as jnp
from jax import lax
from jax.experimental import pallas as pl
from jax.experimental.pallas import tpu as pltpu
from jax.sharding import PartitionSpec as P

LN_EPS = 1e-6
K0 = math.sqrt(2.0 / math.pi)
K1 = K0 * 0.044715
MESH = pl.DeviceIdType.MESH
ANY = pl.BlockSpec(memory_space=pl.ANY)
VMEM = pl.BlockSpec(memory_space=pltpu.VMEM)
USLOTS = 4


def layer_norm(rows_wide, scale, offset):
    mean = jnp.mean(rows_wide, axis=-1, keepdims=True)
    centered = rows_wide - mean
    var = jnp.mean(centered * centered, axis=-1, keepdims=True)
    return (centered * lax.rsqrt(var + LN_EPS) * scale + offset).astype(jnp.bfloat16)


def gelu(a):
    half = a * 0.5
    return half * jnp.tanh(a * ((a * a) * K1 + K0)) + half


def dot(a, b):
    return jnp.dot(a, b, preferred_element_type=jnp.float32)


def rows(start, size, align):
    return pl.ds(pl.multiple_of(start, align), size)


def exchange_kernel(side, x_hbm, s1_ref, o1_ref, wt1_hbm, bt1_ref, wt2_hbm, bt2_hbm,
                    g_out, wt2t_ref, bt2c_ref,
                    xbuf, usend, ubuf, hbuf, ra1, ra2, rb1, rb2, gbuf, wt1, wt1t, wt2, bt2, b1c,
                    ssem, rsem, xsem, wsem, osem, credit):
    B, S, C = x_hbm.shape
    pairs = B // 2
    D = wt1_hbm.shape[1]
    DA, DB, CB = D // side, D // side // 2, C // 2

    me = lax.axis_index("sp")
    core = me % 2
    chip = me // 2
    cx, cy = chip % side, chip // side
    a = cx * (1 - core) + cy * core
    b = cy * (1 - core) + cx * core

    def index(ia, ib):
        ix = ia * (1 - core) + ib * core
        iy = ib * (1 - core) + ia * core
        return (iy * side + ix) * 2 + core

    ar, al, ao = (a + 1) % side, (a + side - 1) % side, (a + 2) % side
    br, bl, bo = (b + 1) % side, (b + side - 1) % side, (b + 2) % side
    dev_ar, dev_al = index(ar, b), index(al, b)
    dev_br, dev_bl = index(a, br), index(a, bl)
    partner = me + 1 - 2 * core

    def remote(k, p, src, dst, dev):
        return pltpu.make_async_remote_copy(
            src_ref=src, dst_ref=dst, send_sem=ssem.at[k, p], recv_sem=rsem.at[k, p],
            device_id={"sp": dev}, device_id_type=MESH)

    def sub(j, off=0, size=None):
        return (rows(a * DA + (j // 2) * DB + off, size or DB, 8), rows((j % 2) * CB, CB, 128))

    mine = core

    def d_u(p):
        return remote(0, p, usend.at[p % 2], ubuf.at[p % USLOTS, rows(core * S, S, 16)], partner)

    def d_a1(p):
        return (remote(1, p, hbuf.at[p, rows(ao * DA, DB, 8)], ra1.at[p, 0], dev_ar),
                remote(2, p, hbuf.at[p, rows(ao * DA + DB, DB, 8)], ra1.at[p, 1], dev_al))

    def d_a2(p):
        return (remote(3, p, hbuf.at[p, rows(ar * DA, DA, 8)], ra2.at[p, 0], dev_ar),
                remote(4, p, hbuf.at[p, rows(al * DA, DA, 8)], ra2.at[p, 1], dev_al))

    def d_b1(p):
        return (remote(5, p, hbuf.at[(p, *sub(bo, 0, DB // 2))], rb1.at[p, 0], dev_br),
                remote(6, p, hbuf.at[(p, *sub(bo, DB // 2, DB // 2))], rb1.at[p, 1], dev_bl))

    def d_b2(p):
        return (remote(7, p, hbuf.at[(p, *sub(br))], rb2.at[p, 0], dev_br),
                remote(8, p, hbuf.at[(p, *sub(bl))], rb2.at[p, 1], dev_bl))

    def d_g1(p):
        here = gbuf.at[(p, mine, *sub(b))]
        return remote(9, p, here, here, dev_br), remote(10, p, here, here, dev_bl)

    def d_g2(p):
        top = gbuf.at[(p, mine, *sub(bl, 0, 32))]
        bottom = gbuf.at[(p, mine, *sub(br, 32, DB - 32))]
        return remote(11, p, top, top, dev_br), remote(12, p, bottom, bottom, dev_bl)

    def d_g3(p):
        here = gbuf.at[p, mine, rows(a * DA, DA, 16)]
        return remote(13, p, here, here, dev_ar), remote(14, p, here, here, dev_al)

    def d_g4(p):
        top = gbuf.at[p, mine, rows(al * DA, DB, 16)]
        bottom = gbuf.at[p, mine, rows(ar * DA + DB, DB, 16)]
        return remote(15, p, top, top, dev_ar), remote(16, p, bottom, bottom, dev_al)

    def d_g5(p):
        here = gbuf.at[p, mine]
        return remote(17, p, here, here, partner)

    def d_x(p):
        return (pltpu.make_async_copy(x_hbm.at[2 * p + 1 - core], xbuf.at[p % 2, 0], xsem.at[p % 2, 0]),
                pltpu.make_async_copy(x_hbm.at[2 * p + core], xbuf.at[p % 2, 1], xsem.at[p % 2, 1]))

    def d_out(p):
        return pltpu.make_async_copy(gbuf.at[p], g_out.at[p], osem.at[p])

    w_copies = (pltpu.make_async_copy(wt1_hbm.at[rows(chip * 2 * S, 2 * S, 16)], wt1, wsem.at[0]),
                pltpu.make_async_copy(wt2_hbm.at[:, rows(me * S, S, 128)], wt2, wsem.at[1]),
                pltpu.make_async_copy(bt2_hbm.at[:, rows(me * S, S, 128)], bt2, wsem.at[2]))

    def start(ds):
        for d in ds:
            d.start()

    def wait_recv(ds):
        for d in ds:
            d.wait_recv()

    LT = min(S, 64)

    def ln1(p):
        @pl.when(p + 1 < pairs)
        def _():
            start(d_x(p + 1))

        other, own = d_x(p)
        other.wait()

        @pl.when(p >= 2)
        def _():
            d_u(p - 2).wait_send()

        @pl.loop(0, S // LT)
        def _(i):
            r = rows(i * LT, LT, LT)
            usend[p % 2, r, :] = layer_norm(xbuf[p % 2, 0, r, :].astype(jnp.float32), s1_ref[...], o1_ref[...])

        @pl.when(p >= USLOTS)
        def _():
            pl.semaphore_wait(credit, 1)

        d_u(p).start()
        own.wait()

        @pl.loop(0, S // LT)
        def _(i):
            r = rows(i * LT, LT, LT)
            ubuf[p % USLOTS, rows(core * S + i * LT, LT, LT), :] = layer_norm(
                xbuf[p % 2, 1, r, :].astype(jnp.float32), s1_ref[...], o1_ref[...])

    def mm1(p):
        d_u(p).wait_recv()
        hbuf[p] = dot(wt1t[...], ubuf[p % USLOTS])

        @pl.when(p + USLOTS < pairs)
        def _():
            pl.semaphore_signal(credit, inc=1, device_id={"sp": partner}, device_id_type=MESH)

        start(d_a1(p))

    def a2(p):
        wait_recv(d_a1(p))
        hbuf[p, rows(ar * DA, DB, 8), :] += ra1[p, 0]
        hbuf[p, rows(al * DA + DB, DB, 8), :] += ra1[p, 1]
        start(d_a2(p))

    def b1(p):
        wait_recv(d_a2(p))
        hbuf[p, rows(a * DA, DA, 8), :] += ra2[p, 0] + ra2[p, 1]
        start(d_b1(p))

    def b2(p):
        wait_recv(d_b1(p))
        hbuf[(p, *sub(br, 0, DB // 2))] += rb1[p, 0]
        hbuf[(p, *sub(bl, DB // 2, DB // 2))] += rb1[p, 1]
        start(d_b2(p))

    def g1(p):
        wait_recv(d_b2(p))
        h = hbuf[(p, *sub(b))] + (rb2[p, 0] + rb2[p, 1])
        bias = b1c[rows(a * DA + (b // 2) * DB, DB, 8), 0:1]
        r, c = sub(b)
        gbuf[p, mine, rows(a * DA + (b // 2) * DB, DB, 16), c] = gelu(h + bias).astype(jnp.bfloat16)
        start(d_g1(p))

    def g2(p):
        wait_recv(d_g1(p))
        start(d_g2(p))

    def g3(p):
        wait_recv(d_g2(p))
        start(d_g3(p))

    def g4(p):
        wait_recv(d_g3(p))
        start(d_g4(p))

    def g5(p):
        wait_recv(d_g4(p))
        d_g5(p).start()

    def g6(p):
        d_g5(p).wait_recv()
        d_out(p).start()

    stages = (ln1, mm1, a2, b1, b2, g1, g2, g3, g4, g5, g6)

    start(w_copies)
    start(d_x(0))
    barrier = pltpu.get_barrier_semaphore()
    neighbours = (dev_ar, dev_al, dev_br, dev_bl, partner)
    for dev in neighbours:
        pl.semaphore_signal(barrier, inc=1, device_id={"sp": dev}, device_id_type=MESH)
    b1c[...] = jnp.transpose(jnp.broadcast_to(bt1_ref[...], (128, D)))
    for w in w_copies:
        w.wait()
    wt1t[...] = jnp.transpose(wt1[...])
    wt2t_ref[...] = jnp.transpose(wt2[...])
    bt2c_ref[...] = jnp.transpose(jnp.broadcast_to(bt2[...], (128, S)))
    pl.semaphore_wait(barrier, len(neighbours))

    @pl.loop(0, pairs + len(stages) - 1)
    def _(t):
        for s in reversed(range(len(stages))):
            @pl.when((t >= s) & (t - s < pairs))
            def _():
                stages[s](t - s)

    for p in (pairs - 2, pairs - 1):
        d_u(p).wait_send()

    @pl.loop(0, pairs)
    def _(p):
        for make in (d_a1, d_a2, d_b1, d_b2, d_g1, d_g2, d_g3, d_g4):
            for d in make(p):
                d.wait_send()
        d_g5(p).wait_send()
        d_out(p).wait()


def exchange(side, patches, s1, o1, w_tok1, b_tok1, w_tok2, b_tok2):
    B, S, C = patches.shape
    pairs = B // 2
    D = w_tok1.shape[1]
    DA, DB, CB = D // side, D // side // 2, C // 2
    f32, bf16 = jnp.float32, jnp.bfloat16
    return pl.pallas_call(
        functools.partial(exchange_kernel, side),
        out_shape=(jax.ShapeDtypeStruct((pairs, 2, D, C), bf16),
                   jax.ShapeDtypeStruct((S, D), bf16),
                   jax.ShapeDtypeStruct((S, 128), f32)),
        in_specs=[ANY, VMEM, VMEM, ANY, VMEM, ANY, ANY],
        out_specs=(ANY, VMEM, VMEM),
        scratch_shapes=[
            pltpu.VMEM((2, 2, S, C), bf16),
            pltpu.VMEM((2, S, C), bf16),
            pltpu.VMEM((USLOTS, 2 * S, C), bf16),
            pltpu.VMEM((pairs, D, C), f32),
            pltpu.VMEM((pairs, 2, DB, C), f32),
            pltpu.VMEM((pairs, 2, DA, C), f32),
            pltpu.VMEM((pairs, 2, DB // 2, CB), f32),
            pltpu.VMEM((pairs, 2, DB, CB), f32),
            pltpu.VMEM((pairs, 2, D, C), bf16),
            pltpu.VMEM((2 * S, D), bf16),
            pltpu.VMEM((D, 2 * S), bf16),
            pltpu.VMEM((D, S), bf16),
            pltpu.VMEM((1, S), f32),
            pltpu.VMEM((D, 128), f32),
            pltpu.SemaphoreType.DMA((18, pairs)),
            pltpu.SemaphoreType.DMA((18, pairs)),
            pltpu.SemaphoreType.DMA((2, 2)),
            pltpu.SemaphoreType.DMA((3,)),
            pltpu.SemaphoreType.DMA((pairs,)),
            pltpu.SemaphoreType.REGULAR,
        ],
        compiler_params=pltpu.CompilerParams(collective_id=0, has_side_effects=True, vmem_limit_bytes=60 << 20),
        name="exchange",
    )(patches, s1, o1, w_tok1, b_tok1, w_tok2, b_tok2)


def mixer_kernel(hc, x_ref, g_ref, wt2_ref, bt2_ref, s2_ref, o2_ref, w1_ref, c1_ref, w2_ref, c2_ref, out_ref,
                 v_scr, q_scr, x1_scr, acc):
    H = w1_ref.shape[1]
    t = (dot(wt2_ref[...], g_ref[0]) + bt2_ref[:, 0:1]).astype(jnp.bfloat16)
    x1 = (x_ref[0].astype(jnp.float32) + t.astype(jnp.float32)).astype(jnp.bfloat16)
    x1_scr[...] = x1
    v_scr[...] = layer_norm(x1.astype(jnp.float32), s2_ref[...], o2_ref[...])
    steps = H // hc
    for c in range(steps + 1):
        if c < steps:
            h = pl.ds(c * hc, hc)
            q_scr[:, h] = gelu(dot(v_scr[...], w1_ref[:, h]) + c1_ref[:, h]).astype(jnp.bfloat16)
        if c >= 1:
            h = pl.ds((c - 1) * hc, hc)
            part = dot(q_scr[:, h], w2_ref[h, :])
            if c == 1:
                acc[...] = part + c2_ref[...]
            elif c < steps:
                acc[...] += part
            else:
                out_ref[0] = (x1_scr[...].astype(jnp.float32) + (acc[...] + part)).astype(jnp.bfloat16)


def mixer(patches, g, wt2t, bt2c, s2, o2, w_ch1, b_ch1, w_ch2, b_ch2):
    B, S, C = patches.shape
    D = g.shape[1]
    H = w_ch1.shape[1]

    def const(*shape):
        return pl.BlockSpec(shape, lambda i: (0,) * len(shape), pipeline_mode=pl.Buffered(1))

    return pl.pallas_call(
        functools.partial(mixer_kernel, min(512, H // 2)),
        grid=(B,),
        in_specs=[pl.BlockSpec((1, S, C), lambda i: (i, 0, 0)), pl.BlockSpec((1, D, C), lambda i: (i, 0, 0)),
                  const(S, D), const(S, 128), const(1, C), const(1, C), const(C, H), const(1, H), const(H, C), const(1, C)],
        out_specs=pl.BlockSpec((1, S, C), lambda i: (i, 0, 0)),
        out_shape=jax.ShapeDtypeStruct((B, S, C), jnp.bfloat16),
        scratch_shapes=[pltpu.VMEM((S, C), jnp.bfloat16), pltpu.VMEM((S, H), jnp.bfloat16),
                        pltpu.VMEM((S, C), jnp.bfloat16), pltpu.VMEM((S, C), jnp.float32)],
        compiler_params=pltpu.CompilerParams(vmem_limit_bytes=60 << 20),
        name="mixer",
    )(patches, g, wt2t, bt2c, s2, o2, w_ch1, b_ch1, w_ch2, b_ch2)


def solution(mesh):
    row_spec = P('dp', 'sp', None)
    side = math.isqrt(mesh.shape['sp'] // 2)

    def local_layer(patches, ln1_scale, ln1_bias, w_tok1, b_tok1, w_tok2, b_tok2, ln2_scale, ln2_bias, w_ch1, b_ch1, w_ch2, b_ch2):
        B, S, C = patches.shape
        g, wt2t, bt2c = exchange(side, patches, ln1_scale[None], ln1_bias[None], w_tok1, b_tok1[None], w_tok2, b_tok2[None])
        return mixer(patches, g.reshape(B, -1, C), wt2t, bt2c, ln2_scale[None], ln2_bias[None],
                     w_ch1, b_ch1[None], w_ch2, b_ch2[None])

    return jax.shard_map(local_layer, mesh=mesh, in_specs=(row_spec,) + (P(),) * 12, out_specs=row_spec, check_vma=False)
```

time: 965 us -> 241 us (0.25); the launches traced: 952 us -> 238 us
  local copies, waits for them, and re-layouts: 428 us -> 7.64 us
  blocking collectives: 322 us -> 0 us
  Pallas kernels: 0 us -> 230 us
  matrix products: 142 us -> 0 us
  other arithmetic: 59.4 us -> 0 us
    all_to_all x2 -> x0, blocking collectives: 322 us -> none  [the longest x1 166 us: local_layer(): normed_cols = lax.all_to_all(normed, 'sp', 2, 1, tiled=True)]
    pallas_call x0 -> x2, Pallas kernels: none -> 230 us  [the longest x1 120 us: exchange(): pl.pallas_call(functools.partial(exchange_kernel, side), out_shape=(jax.S...]
    unnamed x19 -> x0, local copies, waits for them, and re-layouts: 207 us -> none
    dot_general x4 -> x0, matrix products: 142 us -> none  [the longest x1 65.1 us: channel_mixing(): jnp.einsum('bsc,ce->bse', chan_in, w_ch1, preferred_element_type=jnp.floa...]
    convert_element_type x4 -> x0, local copies, waits for them, and re-layouts: 125 us -> none  [the longest x1 56 us: local_layer(): mixed_cols = (mixed + b_tok2[None, :, None]).astype(jnp.bfloat16)]
    all_to_all x3 -> x0, local copies, waits for them, and re-layouts: 96.8 us -> none  [the longest x1 58 us: local_layer(): mixed_rows = lax.all_to_all(mixed_cols, 'sp', 1, 2, tiled=True)]
    reduce_sum x4 -> x0, other arithmetic: 40.3 us -> none  [the longest x2 24 us: layer_norm(): row_mean = jnp.mean(rows_wide, axis=-1, keepdims=True)]
    convert_element_type x2 -> x0, other arithmetic: 19 us -> none  [the longest x1 12.5 us: layer_norm(): (centered * lax.rsqrt(row_var + LN_EPS) * scale + offset).astype(jnp.bflo...]
where the time goes in v1:
time: 241 us; the launch traced here: 238 us
  Pallas kernels  230 us (95%)
  local copies, waits for them, and re-layouts  7.64 us (3%)
    pallas_call x1, Pallas kernels, exchange(): pl.pallas_call(functools.partial(exchange_kernel, side), out_shape=(jax.S...  120 us
    pallas_call x1, Pallas kernels, mixer(): pl.pallas_call(functools.partial(mixer_kernel, min(512, H // 2)), grid=(B...  110 us

profile of v1, /device:TPU:96, one launch (start us, length us, event | category | flops | bytes accessed | tf_op | source)
XLA Modules:
  0.0 237.5 jit_solution(17688553931374431498)
XLA Ops:
  0.0 1.3 broadcast_in_dim.26.bt1_ref
  1.3 1.3 broadcast_in_dim.24.s1_ref
  2.5 1.3 broadcast_in_dim.25.o1_ref
  3.8 1.3 broadcast_in_dim.28.s2_ref
  5.1 1.3 broadcast_in_dim.29.o2_ref
  6.4 1.3 broadcast_in_dim.31.c2_ref
  7.6 120.2 %exchange.1 = (bf16[8,2,384,768]{3,2,1,0:T(8,128)(2,1)}, bf16[512,384]{1,0:T(8,128)(2,1)}, f32[512,128]{1,0:T(8,128)}) custom-call(bf16[16,512,768]{2,1,0:T(8,128)(2,1)} %x_ref.1, f32[1,768]{1,0:T(1,128)} %broadcast_in_dim.24.s1_ref, f32[1,768]{1,0:T(1,128)} %broadcast_in_dim.25.o1_ref, bf16[16384,384]{1,0:T(8,128)(2,1)} %wt1_hbm.1, ...), custom_call_target="tpu_custom_call" | custom-call | tf_op jit(solution)/shard_map/exchange/pallas_call | solution.py:265
  127.9 109.7 %mixer.1 = bf16[16,512,768]{2,1,0:T(8,128)(2,1)} custom-call(bf16[16,512,768]{2,1,0:T(8,128)(2,1)} %x_ref.1, bf16[16,384,768]{2,1,0:T(8,128)(2,1)} %bitcast.3, bf16[512,384]{1,0:T(8,128)(2,1)} %get-tuple-element.9.wt2_ref, f32[512,128]{1,0:T(8,128)} %get-tuple-element.10.bt2_ref, f32[1,768]{1,0:T(1,128)} %broadcast_in_dim.28.s2_ref, ...), custom_call_target="tpu_custom_call" | custom-call | tf_op jit(solution)/shard_map/mixer/pallas_call | solution.py:330

commit v2 on v1

--- a/solution.py
+++ b/solution.py
@@ -15,6 +15,9 @@
 ANY = pl.BlockSpec(memory_space=pl.ANY)
 VMEM = pl.BlockSpec(memory_space=pltpu.VMEM)
 USLOTS = 4
+FIRST, PERIOD = 9, 4
+A1, A2, B1, B2 = (1, -1), (2, 0), (3, 2), (4, 3)
+G1, G2, G3, G4, G5, G6 = (5, 4), (6, 5), (7, 6), (8, 7), (9, 8), (11, 9)
 
 
 def layer_norm(rows_wide, scale, offset):
@@ -33,14 +36,20 @@
     return jnp.dot(a, b, preferred_element_type=jnp.float32)
 
 
+def row(ref, cols=slice(None)):
+    return ref[cols][None, :]
+
+
 def rows(start, size, align):
     return pl.ds(pl.multiple_of(start, align), size)
 
 
-def exchange_kernel(side, x_hbm, s1_ref, o1_ref, wt1_hbm, bt1_ref, wt2_hbm, bt2_hbm,
-                    g_out, wt2t_ref, bt2c_ref,
-                    xbuf, usend, ubuf, hbuf, ra1, ra2, rb1, rb2, gbuf, wt1, wt1t, wt2, bt2, b1c,
-                    ssem, rsem, xsem, wsem, osem, credit):
+def exchange_kernel(side, done_pairs, x_hbm, s1_ref, o1_ref, wt1_hbm, bt1_ref, wt2_hbm, bt2_hbm,
+                    s2_ref, o2_ref, w1_hbm, c1_ref, w2_hbm, c2_ref,
+                    out_hbm, g_out, wt2t_ref, bt2c_ref,
+                    xbuf, usend, ubuf, hbuf, ra1, ra2, rb1, rb2, gbuf, wt1t, wt2, bt2, b1c,
+                    w1, w2, xres, obuf, v_scr, q_scr, x1_scr, acc,
+                    ssem, rsem, xsem, wsem, osem, xrsem, obsem, credit):
     B, S, C = x_hbm.shape
     pairs = B // 2
     D = wt1_hbm.shape[1]
@@ -120,8 +129,10 @@
                 pltpu.make_async_copy(x_hbm.at[2 * p + core], xbuf.at[p % 2, 1], xsem.at[p % 2, 1]))
 
     def d_out(p):
-        return pltpu.make_async_copy(gbuf.at[p], g_out.at[p], osem.at[p])
-
+        return pltpu.make_async_copy(gbuf.at[p], g_out.at[p - done_pairs], osem.at[p - done_pairs])
+
+    wt1 = ubuf.at[USLOTS - 1, :, pl.ds(0, D)] if D <= C else None
+    ch_copies = (pltpu.make_async_copy(w1_hbm, w1, wsem.at[3]), pltpu.make_async_copy(w2_hbm, w2, wsem.at[4]))
     w_copies = (pltpu.make_async_copy(wt1_hbm.at[rows(chip * 2 * S, 2 * S, 16)], wt1, wsem.at[0]),
                 pltpu.make_async_copy(wt2_hbm.at[:, rows(me * S, S, 128)], wt2, wsem.at[1]),
                 pltpu.make_async_copy(bt2_hbm.at[:, rows(me * S, S, 128)], bt2, wsem.at[2]))
@@ -151,7 +162,7 @@
         @pl.loop(0, S // LT)
         def _(i):
             r = rows(i * LT, LT, LT)
-            usend[p % 2, r, :] = layer_norm(xbuf[p % 2, 0, r, :].astype(jnp.float32), s1_ref[...], o1_ref[...])
+            usend[p % 2, r, :] = layer_norm(xbuf[p % 2, 0, r, :].astype(jnp.float32), row(s1_ref), row(o1_ref))
 
         @pl.when(p >= USLOTS)
         def _():
@@ -164,7 +175,7 @@
         def _(i):
             r = rows(i * LT, LT, LT)
             ubuf[p % USLOTS, rows(core * S + i * LT, LT, LT), :] = layer_norm(
-                xbuf[p % 2, 1, r, :].astype(jnp.float32), s1_ref[...], o1_ref[...])
+                xbuf[p % 2, 1, r, :].astype(jnp.float32), row(s1_ref), row(o1_ref))
 
     def mm1(p):
         d_u(p).wait_recv()
@@ -174,6 +185,7 @@
         def _():
             pl.semaphore_signal(credit, inc=1, device_id={"sp": partner}, device_id_type=MESH)
 
+    def a1(p):
         start(d_a1(p))
 
     def a2(p):
@@ -219,9 +231,43 @@
 
     def g6(p):
         d_g5(p).wait_recv()
-        d_out(p).start()
-
-    stages = (ln1, mm1, a2, b1, b2, g1, g2, g3, g4, g5, g6)
+
+        @pl.when(p >= done_pairs)
+        def _():
+            d_out(p).start()
+
+    plan = ((g6, G6[0], G6[1]), (g5, G5[0], G5[1]), (g4, G4[0], G4[1]), (g3, G3[0], G3[1]), (g2, G2[0], G2[1]),
+            (g1, G1[0], G1[1]), (b2, B2[0], B2[1]), (b1, B1[0], B1[1]), (a2, A2[0], A2[1]), (a1, A1[0], A1[1]))
+
+    def slot(t, parity=None):
+        for n, (stage, first, later) in enumerate(plan):
+            if parity is not None and (later - parity) % 2 and (first < FIRST or (first - parity) % 2):
+                continue
+            if parity is None and n == len(plan) - 1:
+                prepare(t)
+            q = t + PERIOD * pairs - later
+            p = q // PERIOD - pairs
+            late = (q % PERIOD == 0) & (p >= 1) & (p < pairs)
+
+            @pl.when(late | (t == first))
+            def _():
+                stage(jnp.where(late, p, 0))
+
+    def prepare(t):
+        @pl.when((t >= 1) & (t <= pairs))
+        def _():
+            mm1(t - 1)
+
+    def image_of(k):
+        return core + (k % 2) * (1 - 2 * core)
+
+    def d_res(k):
+        return pltpu.make_async_copy(x_hbm.at[(k // 2) * 2 + image_of(k)], xres.at[k % 2], xrsem.at[k % 2])
+
+    def d_done(k):
+        return pltpu.make_async_copy(obuf.at[k % 2], out_hbm.at[(k // 2) * 2 + image_of(k)], obsem.at[k % 2])
+
+    mlp = functools.partial(mlp_half, wt2t_ref, bt2c_ref, s2_ref, o2_ref, w1, c1_ref, w2, c2_ref, v_scr, q_scr, x1_scr, acc)
 
     start(w_copies)
     start(d_x(0))
@@ -229,21 +275,56 @@
     neighbours = (dev_ar, dev_al, dev_br, dev_bl, partner)
     for dev in neighbours:
         pl.semaphore_signal(barrier, inc=1, device_id={"sp": dev}, device_id_type=MESH)
-    b1c[...] = jnp.transpose(jnp.broadcast_to(bt1_ref[...], (128, D)))
+    b1c[...] = jnp.transpose(jnp.broadcast_to(row(bt1_ref), (128, D)))
     for w in w_copies:
         w.wait()
+    start(ch_copies)
+    d_res(0).start()
     wt1t[...] = jnp.transpose(wt1[...])
-    wt2t_ref[...] = jnp.transpose(wt2[...])
-    bt2c_ref[...] = jnp.transpose(jnp.broadcast_to(bt2[...], (128, S)))
     pl.semaphore_wait(barrier, len(neighbours))
-
-    @pl.loop(0, pairs + len(stages) - 1)
+    steps = 2 * done_pairs
+
+    @pl.loop(0, FIRST)
     def _(t):
-        for s in reversed(range(len(stages))):
-            @pl.when((t >= s) & (t - s < pairs))
-            def _():
-                stages[s](t - s)
-
+        slot(t)
+
+        @pl.when(t < pairs)
+        def _():
+            ln1(t)
+
+        @pl.when(t == 0)
+        def _():
+            wt2t_ref[...] = jnp.transpose(wt2[...])
+            bt2c_ref[...] = jnp.transpose(jnp.broadcast_to(bt2[...], (128, S)))
+
+    for w in ch_copies:
+        w.wait()
+
+    @pl.loop(0, steps)
+    def _(k):
+        slot(FIRST + 2 * k, FIRST % 2)
+
+        @pl.when(k + 1 < steps)
+        def _():
+            d_res(k + 1).start()
+
+        d_res(k).wait()
+        mlp(0, xres.at[k % 2], gbuf.at[k // 2, image_of(k)], None)
+        slot(FIRST + 2 * k + 1, (FIRST + 1) % 2)
+
+        @pl.when(k >= 2)
+        def _():
+            d_done(k - 2).wait()
+
+        mlp(1, None, None, obuf.at[k % 2])
+        d_done(k).start()
+
+    @pl.loop(FIRST + 2 * steps, G6[1] + PERIOD * (pairs - 1) + 1)
+    def _(t):
+        slot(t)
+
+    d_done(steps - 2).wait()
+    d_done(steps - 1).wait()
     for p in (pairs - 2, pairs - 1):
         d_u(p).wait_send()
 
@@ -253,22 +334,54 @@
             for d in make(p):
                 d.wait_send()
         d_g5(p).wait_send()
+
+    @pl.loop(done_pairs, pairs)
+    def _(p):
         d_out(p).wait()
 
 
-def exchange(side, patches, s1, o1, w_tok1, b_tok1, w_tok2, b_tok2):
+def mlp_half(wt2t, bt2c, s2, o2, w1, c1, w2, c2, v_scr, q_scr, x1_scr, acc, half, x, g, out):
+    H, hc = w1.shape[1], q_scr.shape[2]
+    steps = H // hc
+    if half == 0:
+        t = (dot(wt2t[...], g[...]) + bt2c[:, 0:1]).astype(jnp.bfloat16)
+        x1 = (x[...].astype(jnp.float32) + t.astype(jnp.float32)).astype(jnp.bfloat16)
+        x1_scr[...] = x1
+        v_scr[...] = layer_norm(x1.astype(jnp.float32), row(s2), row(o2))
+    for c in range(0, steps // 2) if half == 0 else range(steps // 2, steps + 1):
+        if c < steps:
+            h = pl.ds(c * hc, hc)
+            q_scr[c % 2] = gelu(dot(v_scr[...], w1[:, h]) + row(c1, h)).astype(jnp.bfloat16)
+        if c >= 1:
+            part = dot(q_scr[(c - 1) % 2], w2[pl.ds((c - 1) * hc, hc), :])
+            if c == 1:
+                acc[...] = part + row(c2)
+            elif c < steps:
+                acc[...] += part
+            else:
+                out[...] = (x1_scr[...].astype(jnp.float32) + (acc[...] + part)).astype(jnp.bfloat16)
+
+
+def mlp_scratch(S, C, H):
+    hc = min(512, H // 2)
+    return [pltpu.VMEM((S, C), jnp.bfloat16), pltpu.VMEM((2, S, hc), jnp.bfloat16),
+            pltpu.VMEM((S, C), jnp.bfloat16), pltpu.VMEM((S, C), jnp.float32)]
+
+
+def exchange(side, done_pairs, patches, s1, o1, w_tok1, b_tok1, w_tok2, b_tok2, s2, o2, w_ch1, b_ch1, w_ch2, b_ch2):
     B, S, C = patches.shape
     pairs = B // 2
-    D = w_tok1.shape[1]
+    D, H = w_tok1.shape[1], w_ch1.shape[1]
     DA, DB, CB = D // side, D // side // 2, C // 2
     f32, bf16 = jnp.float32, jnp.bfloat16
     return pl.pallas_call(
-        functools.partial(exchange_kernel, side),
-        out_shape=(jax.ShapeDtypeStruct((pairs, 2, D, C), bf16),
+        functools.partial(exchange_kernel, side, done_pairs),
+        out_shape=(jax.ShapeDtypeStruct((2 * done_pairs, S, C), bf16),
+                   jax.ShapeDtypeStruct((pairs - done_pairs, 2, D, C), bf16),
                    jax.ShapeDtypeStruct((S, D), bf16),
                    jax.ShapeDtypeStruct((S, 128), f32)),
-        in_specs=[ANY, VMEM, VMEM, ANY, VMEM, ANY, ANY],
-        out_specs=(ANY, VMEM, VMEM),
+        in_specs=[ANY, VMEM, VMEM, ANY, VMEM, ANY, ANY, VMEM, VMEM, ANY, VMEM, ANY, VMEM],
+        out_specs=(ANY, ANY, VMEM, VMEM),
         scratch_shapes=[
             pltpu.VMEM((2, 2, S, C), bf16),
             pltpu.VMEM((2, S, C), bf16),
@@ -279,66 +392,81 @@
             pltpu.VMEM((pairs, 2, DB // 2, CB), f32),
             pltpu.VMEM((pairs, 2, DB, CB), f32),
             pltpu.VMEM((pairs, 2, D, C), bf16),
-            pltpu.VMEM((2 * S, D), bf16),
             pltpu.VMEM((D, 2 * S), bf16),
             pltpu.VMEM((D, S), bf16),
             pltpu.VMEM((1, S), f32),
             pltpu.VMEM((D, 128), f32),
+            pltpu.VMEM((C, H), bf16),
+            pltpu.VMEM((H, C), bf16),
+            pltpu.VMEM((2, S, C), bf16),
+            pltpu.VMEM((2, S, C), bf16),
+            *mlp_scratch(S, C, H),
             pltpu.SemaphoreType.DMA((18, pairs)),
             pltpu.SemaphoreType.DMA((18, pairs)),
             pltpu.SemaphoreType.DMA((2, 2)),
-            pltpu.SemaphoreType.DMA((3,)),
-            pltpu.SemaphoreType.DMA((pairs,)),
+            pltpu.SemaphoreType.DMA((5,)),
+            pltpu.SemaphoreType.DMA((pairs - done_pairs,)),
+            pltpu.SemaphoreType.DMA((2,)),
+            pltpu.SemaphoreType.DMA((2,)),
             pltpu.SemaphoreType.REGULAR,
         ],
-        compiler_params=pltpu.CompilerParams(collective_id=0, has_side_effects=True, vmem_limit_bytes=60 << 20),
+        compiler_params=pltpu.CompilerParams(collective_id=0, has_side_effects=True, vmem_limit_bytes=67043328),
         name="exchange",
-    )(patches, s1, o1, w_tok1, b_tok1, w_tok2, b_tok2)
-
-
-def mixer_kernel(hc, x_ref, g_ref, wt2_ref, bt2_ref, s2_ref, o2_ref, w1_ref, c1_ref, w2_ref, c2_ref, out_ref,
-                 v_scr, q_scr, x1_scr, acc):
-    H = w1_ref.shape[1]
-    t = (dot(wt2_ref[...], g_ref[0]) + bt2_ref[:, 0:1]).astype(jnp.bfloat16)
-    x1 = (x_ref[0].astype(jnp.float32) + t.astype(jnp.float32)).astype(jnp.bfloat16)
-    x1_scr[...] = x1
-    v_scr[...] = layer_norm(x1.astype(jnp.float32), s2_ref[...], o2_ref[...])
-    steps = H // hc
-    for c in range(steps + 1):
-        if c < steps:
-            h = pl.ds(c * hc, hc)
-            q_scr[:, h] = gelu(dot(v_scr[...], w1_ref[:, h]) + c1_ref[:, h]).astype(jnp.bfloat16)
-        if c >= 1:
-            h = pl.ds((c - 1) * hc, hc)
-            part = dot(q_scr[:, h], w2_ref[h, :])
-            if c == 1:
-                acc[...] = part + c2_ref[...]
-            elif c < steps:
-                acc[...] += part
-            else:
-                out_ref[0] = (x1_scr[...].astype(jnp.float32) + (acc[...] + part)).astype(jnp.bfloat16)
-
-
-def mixer(patches, g, wt2t, bt2c, s2, o2, w_ch1, b_ch1, w_ch2, b_ch2):
+    )(patches, s1, o1, w_tok1, b_tok1, w_tok2, b_tok2, s2, o2, w_ch1, b_ch1, w_ch2, b_ch2)
+
+
+def finish_kernel(x_hbm, early_hbm, g_hbm, wt2t, bt2c, s2, o2, w1_hbm, c1, w2_hbm, c2, out_hbm,
+                  carry, xbuf, gbuf, obuf, w1, w2, v_scr, q_scr, x1_scr, acc, csem, dsem, xsem, gsem, osem, wsem):
+    early, rest = carry.shape[0], xbuf.shape[0]
+    w_copies = (pltpu.make_async_copy(w1_hbm, w1, wsem.at[0]), pltpu.make_async_copy(w2_hbm, w2, wsem.at[1]))
+    xs = [pltpu.make_async_copy(x_hbm.at[early + i], xbuf.at[i], xsem.at[i]) for i in range(rest)]
+    gs = [pltpu.make_async_copy(g_hbm.at[i // 2, i % 2], gbuf.at[i], gsem.at[i]) for i in range(rest)]
+    outs = [pltpu.make_async_copy(obuf.at[i], out_hbm.at[early + i], osem.at[i]) for i in range(rest)]
+    ins = [pltpu.make_async_copy(early_hbm.at[i], carry.at[i], csem.at[i]) for i in range(early)]
+    backs = [pltpu.make_async_copy(carry.at[i], out_hbm.at[i], dsem.at[i]) for i in range(early)]
+    for i in range(rest):
+        xs[i].start()
+        gs[i].start()
+        if i == 0:
+            w_copies[0].start()
+            w_copies[1].start()
+    for c in ins:
+        c.start()
+    mlp = functools.partial(mlp_half, wt2t, bt2c, s2, o2, w1, c1, w2, c2, v_scr, q_scr, x1_scr, acc)
+    for i in range(rest):
+        xs[i].wait()
+        gs[i].wait()
+        if i == 0:
+            w_copies[0].wait()
+            w_copies[1].wait()
+        mlp(0, xbuf.at[i], gbuf.at[i], None)
+        if i == 0:
+            for c, d in zip(ins, backs):
+                c.wait()
+                d.start()
+        mlp(1, None, None, obuf.at[i])
+        outs[i].start()
+    for c in (*backs, *outs):
+        c.wait()
+
+
+def finish(patches, early, g, wt2t, bt2c, s2, o2, w_ch1, b_ch1, w_ch2, b_ch2):
     B, S, C = patches.shape
-    D = g.shape[1]
-    H = w_ch1.shape[1]
-
-    def const(*shape):
-        return pl.BlockSpec(shape, lambda i: (0,) * len(shape), pipeline_mode=pl.Buffered(1))
-
+    D, H = g.shape[2], w_ch1.shape[1]
+    n, rest = early.shape[0], B - early.shape[0]
+    bf16 = jnp.bfloat16
+    dma = pltpu.SemaphoreType.DMA
     return pl.pallas_call(
-        functools.partial(mixer_kernel, min(512, H // 2)),
-        grid=(B,),
-        in_specs=[pl.BlockSpec((1, S, C), lambda i: (i, 0, 0)), pl.BlockSpec((1, D, C), lambda i: (i, 0, 0)),
-                  const(S, D), const(S, 128), const(1, C), const(1, C), const(C, H), const(1, H), const(H, C), const(1, C)],
-        out_specs=pl.BlockSpec((1, S, C), lambda i: (i, 0, 0)),
-        out_shape=jax.ShapeDtypeStruct((B, S, C), jnp.bfloat16),
-        scratch_shapes=[pltpu.VMEM((S, C), jnp.bfloat16), pltpu.VMEM((S, H), jnp.bfloat16),
-                        pltpu.VMEM((S, C), jnp.bfloat16), pltpu.VMEM((S, C), jnp.float32)],
+        finish_kernel,
+        in_specs=[ANY, ANY, ANY, VMEM, VMEM, VMEM, VMEM, ANY, VMEM, ANY, VMEM],
+        out_specs=ANY,
+        out_shape=jax.ShapeDtypeStruct((B, S, C), bf16),
+        scratch_shapes=[pltpu.VMEM((n, S, C), bf16), pltpu.VMEM((rest, S, C), bf16), pltpu.VMEM((rest, D, C), bf16),
+                        pltpu.VMEM((rest, S, C), bf16), pltpu.VMEM((C, H), bf16), pltpu.VMEM((H, C), bf16),
+                        *mlp_scratch(S, C, H), dma((n,)), dma((n,)), dma((rest,)), dma((rest,)), dma((rest,)), dma((2,))],
         compiler_params=pltpu.CompilerParams(vmem_limit_bytes=60 << 20),
-        name="mixer",
-    )(patches, g, wt2t, bt2c, s2, o2, w_ch1, b_ch1, w_ch2, b_ch2)
+        name="finish",
+    )(patches, early, g, wt2t, bt2c, s2, o2, w_ch1, b_ch1, w_ch2, b_ch2)
 
 
 def solution(mesh):
@@ -346,9 +474,9 @@
     side = math.isqrt(mesh.shape['sp'] // 2)
 
     def local_layer(patches, ln1_scale, ln1_bias, w_tok1, b_tok1, w_tok2, b_tok2, ln2_scale, ln2_bias, w_ch1, b_ch1, w_ch2, b_ch2):
-        B, S, C = patches.shape
-        g, wt2t, bt2c = exchange(side, patches, ln1_scale[None], ln1_bias[None], w_tok1, b_tok1[None], w_tok2, b_tok2[None])
-        return mixer(patches, g.reshape(B, -1, C), wt2t, bt2c, ln2_scale[None], ln2_bias[None],
-                     w_ch1, b_ch1[None], w_ch2, b_ch2[None])
+        tail = (ln2_scale, ln2_bias, w_ch1, b_ch1, w_ch2, b_ch2)
+        early, g, wt2t, bt2c = exchange(side, patches.shape[0] // 2 - 1, patches, ln1_scale, ln1_bias, w_tok1, b_tok1,
+                                        w_tok2, b_tok2[None], *tail)
+        return finish(patches, early, g, wt2t, bt2c, *tail)
 
     return jax.shard_map(local_layer, mesh=mesh, in_specs=(row_spec,) + (P(),) * 12, out_specs=row_spec, check_vma=False)

time: 241 us -> 203 us (0.84); the launches traced: 238 us -> 202 us
  Pallas kernels: 230 us -> 202 us
  local copies, waits for them, and re-layouts: 7.64 us -> 0 us
    pallas_call x2, Pallas kernels: 230 us -> 202 us  [the longest x1 179 us: exchange(): pl.pallas_call(functools.partial(exchange_kernel, side, done_pairs), out_...]
    broadcast_in_dim x6 -> x0, local copies, waits for them, and re-layouts: 7.64 us -> none  [the longest x1 1.28 us: local_layer(): b_ch2[None]]
where the time goes in v2:
time: 203 us; the launch traced here: 202 us
  Pallas kernels  202 us (100%)
    pallas_call x1, Pallas kernels, exchange(): pl.pallas_call(functools.partial(exchange_kernel, side, done_pairs), out_...  179 us
    pallas_call x1, Pallas kernels, finish(): pl.pallas_call(finish_kernel, in_specs=[ANY, ANY, ANY, VMEM, VMEM, VMEM,...  23.1 us

profile of v2, /device:TPU:96, one launch (start us, length us, event | category | flops | bytes accessed | tf_op | source)
XLA Modules:
  0.0 202.4 jit_solution(740144212577777284)
XLA Ops:
  0.0 179.1 %exchange.1 = (bf16[14,512,768]{2,1,0:T(8,128)(2,1)}, bf16[1,2,384,768]{3,2,1,0:T(8,128)(2,1)}, bf16[512,384]{1,0:T(8,128)(2,1)}, f32[512,128]{1,0:T(8,128)}) custom-call(bf16[16,512,768]{2,1,0:T(8,128)(2,1)} %x_hbm.3, f32[768]{0:T(1024)} %s1_ref.1, f32[768]{0:T(1024)} %o1_ref.1, bf16[16384,384]{1,0:T(8,128)(2,1)} %wt1_hbm.1, f32[384]{0:T(512)} %bt1_ref.1, ...), custom_call_target="tpu_custom_call" | custom-call | tf_op jit(solution)/shard_map/exchange/pallas_call | solution.py:377
  179.1 23.1 %finish.1 = bf16[16,512,768]{2,1,0:T(8,128)(2,1)} custom-call(bf16[16,512,768]{2,1,0:T(8,128)(2,1)} %x_hbm.3, bf16[14,512,768]{2,1,0:T(8,128)(2,1)} %get-tuple-element.9.early_hbm, bf16[1,2,384,768]{3,2,1,0:T(8,128)(2,1)} %get-tuple-element.10.g_hbm, bf16[512,384]{1,0:T(8,128)(2,1)} %get-tuple-element.11.wt2t, f32[512,128]{1,0:T(8,128)} %get-tuple-element.12.bt2c, ...), custom_call_target="tpu_custom_call" | custom-call | tf_op jit(solution)/shard_map/finish/pallas_call | solution.py:459

commit v3 on v2

--- a/solution.py
+++ b/solution.py
@@ -15,9 +15,9 @@
 ANY = pl.BlockSpec(memory_space=pl.ANY)
 VMEM = pl.BlockSpec(memory_space=pltpu.VMEM)
 USLOTS = 4
-FIRST, PERIOD = 9, 4
-A1, A2, B1, B2 = (1, -1), (2, 0), (3, 2), (4, 3)
-G1, G2, G3, G4, G5, G6 = (5, 4), (6, 5), (7, 6), (8, 7), (9, 8), (11, 9)
+FIRST, PERIOD = 7, 4
+A1, A2, B1 = (None, 2, -5), (2, 4, -3), (3, 6, -1)
+G1, G3, G4, G5, G6 = (4, 7, 1), (5, 8, 3), (6, 10, 5), (7, 11, 6), (9, 13, 7)
 
 
 def layer_norm(rows_wide, scale, offset):
@@ -47,7 +47,7 @@
 def exchange_kernel(side, done_pairs, x_hbm, s1_ref, o1_ref, wt1_hbm, bt1_ref, wt2_hbm, bt2_hbm,
                     s2_ref, o2_ref, w1_hbm, c1_ref, w2_hbm, c2_ref,
                     out_hbm, g_out, wt2t_ref, bt2c_ref,
-                    xbuf, usend, ubuf, hbuf, ra1, ra2, rb1, rb2, gbuf, wt1t, wt2, bt2, b1c,
+                    xbuf, usend, ubuf, hbuf, ra1, ra2, rb, gbuf, wt1t, wt2, bt2, b1c,
                     w1, w2, xres, obuf, v_scr, q_scr, x1_scr, acc,
                     ssem, rsem, xsem, wsem, osem, xrsem, obsem, credit):
     B, S, C = x_hbm.shape
@@ -70,7 +70,7 @@
     ar, al, ao = (a + 1) % side, (a + side - 1) % side, (a + 2) % side
     br, bl, bo = (b + 1) % side, (b + side - 1) % side, (b + 2) % side
     dev_ar, dev_al = index(ar, b), index(al, b)
-    dev_br, dev_bl = index(a, br), index(a, bl)
+    dev_br, dev_bl, dev_bo = index(a, br), index(a, bl), index(a, bo)
     partner = me + 1 - 2 * core
 
     def remote(k, p, src, dst, dev):
@@ -78,8 +78,8 @@
             src_ref=src, dst_ref=dst, send_sem=ssem.at[k, p], recv_sem=rsem.at[k, p],
             device_id={"sp": dev}, device_id_type=MESH)
 
-    def sub(j, off=0, size=None):
-        return (rows(a * DA + (j // 2) * DB + off, size or DB, 8), rows((j % 2) * CB, CB, 128))
+    def sub(j):
+        return (rows(a * DA + (j // 2) * DB, DB, 16), rows((j % 2) * CB, CB, 128))
 
     mine = core
 
@@ -95,34 +95,25 @@
                 remote(4, p, hbuf.at[p, rows(al * DA, DA, 8)], ra2.at[p, 1], dev_al))
 
     def d_b1(p):
-        return (remote(5, p, hbuf.at[(p, *sub(bo, 0, DB // 2))], rb1.at[p, 0], dev_br),
-                remote(6, p, hbuf.at[(p, *sub(bo, DB // 2, DB // 2))], rb1.at[p, 1], dev_bl))
-
-    def d_b2(p):
-        return (remote(7, p, hbuf.at[(p, *sub(br))], rb2.at[p, 0], dev_br),
-                remote(8, p, hbuf.at[(p, *sub(bl))], rb2.at[p, 1], dev_bl))
+        return tuple(remote(5 + i, p, hbuf.at[(p, *sub(j))], rb.at[p, i], dev)
+                     for i, (j, dev) in enumerate(((br, dev_br), (bl, dev_bl), (bo, dev_bo))))
 
     def d_g1(p):
         here = gbuf.at[(p, mine, *sub(b))]
-        return remote(9, p, here, here, dev_br), remote(10, p, here, here, dev_bl)
-
-    def d_g2(p):
-        top = gbuf.at[(p, mine, *sub(bl, 0, 32))]
-        bottom = gbuf.at[(p, mine, *sub(br, 32, DB - 32))]
-        return remote(11, p, top, top, dev_br), remote(12, p, bottom, bottom, dev_bl)
+        return tuple(remote(8 + i, p, here, here, dev) for i, dev in enumerate((dev_br, dev_bl, dev_bo)))
 
     def d_g3(p):
         here = gbuf.at[p, mine, rows(a * DA, DA, 16)]
-        return remote(13, p, here, here, dev_ar), remote(14, p, here, here, dev_al)
+        return remote(11, p, here, here, dev_ar), remote(12, p, here, here, dev_al)
 
     def d_g4(p):
         top = gbuf.at[p, mine, rows(al * DA, DB, 16)]
         bottom = gbuf.at[p, mine, rows(ar * DA + DB, DB, 16)]
-        return remote(15, p, top, top, dev_ar), remote(16, p, bottom, bottom, dev_al)
+        return remote(13, p, top, top, dev_ar), remote(14, p, bottom, bottom, dev_al)
 
     def d_g5(p):
         here = gbuf.at[p, mine]
-        return remote(17, p, here, here, partner)
+        return remote(15, p, here, here, partner)
 
     def d_x(p):
         return (pltpu.make_async_copy(x_hbm.at[2 * p + 1 - core], xbuf.at[p % 2, 0], xsem.at[p % 2, 0]),
@@ -145,7 +136,7 @@
         for d in ds:
             d.wait_recv()
 
-    LT = min(S, 64)
+    LT = min(S, 256)
 
     def ln1(p):
         @pl.when(p + 1 < pairs)
@@ -199,26 +190,15 @@
         hbuf[p, rows(a * DA, DA, 8), :] += ra2[p, 0] + ra2[p, 1]
         start(d_b1(p))
 
-    def b2(p):
+    def g1(p):
         wait_recv(d_b1(p))
-        hbuf[(p, *sub(br, 0, DB // 2))] += rb1[p, 0]
-        hbuf[(p, *sub(bl, DB // 2, DB // 2))] += rb1[p, 1]
-        start(d_b2(p))
-
-    def g1(p):
-        wait_recv(d_b2(p))
-        h = hbuf[(p, *sub(b))] + (rb2[p, 0] + rb2[p, 1])
-        bias = b1c[rows(a * DA + (b // 2) * DB, DB, 8), 0:1]
+        h = (hbuf[(p, *sub(b))] + rb[p, 2]) + (rb[p, 0] + rb[p, 1])
         r, c = sub(b)
-        gbuf[p, mine, rows(a * DA + (b // 2) * DB, DB, 16), c] = gelu(h + bias).astype(jnp.bfloat16)
+        gbuf[p, mine, r, c] = gelu(h + b1c[r, 0:1]).astype(jnp.bfloat16)
         start(d_g1(p))
 
-    def g2(p):
+    def g3(p):
         wait_recv(d_g1(p))
-        start(d_g2(p))
-
-    def g3(p):
-        wait_recv(d_g2(p))
         start(d_g3(p))
 
     def g4(p):
@@ -236,27 +216,43 @@
         def _():
             d_out(p).start()
 
-    plan = ((g6, G6[0], G6[1]), (g5, G5[0], G5[1]), (g4, G4[0], G4[1]), (g3, G3[0], G3[1]), (g2, G2[0], G2[1]),
-            (g1, G1[0], G1[1]), (b2, B2[0], B2[1]), (b1, B1[0], B1[1]), (a2, A2[0], A2[1]), (a1, A1[0], A1[1]))
-
-    def slot(t, parity=None):
-        for n, (stage, first, later) in enumerate(plan):
-            if parity is not None and (later - parity) % 2 and (first < FIRST or (first - parity) % 2):
+    plan = ((g6, G6), (g5, G5), (g4, G4), (g3, G3), (g1, G1), (b1, B1), (a2, A2), (a1, A1))
+
+    def slot(t, parity=None, lead=False):
+        for stage, (first, second, later) in plan:
+            if lead and stage is a1:
+                prepare(t)
+            firsts = [(p, u) for p, u in enumerate((first, second))
+                      if u is not None and (lead == (u < FIRST)) and (lead or parity is None or (u - parity) % 2 == 0)]
+            even = parity is None or (later - parity) % 2 == 0
+            if not even and not firsts:
                 continue
-            if parity is None and n == len(plan) - 1:
-                prepare(t)
-            q = t + PERIOD * pairs - later
-            p = q // PERIOD - pairs
-            late = (q % PERIOD == 0) & (p >= 1) & (p < pairs)
-
-            @pl.when(late | (t == first))
+            due, pair = False, 0
+            if even:
+                q = t + PERIOD * pairs - later
+                p = q // PERIOD - pairs
+                due = (q % PERIOD == 0) & (p >= 2) & (p < pairs)
+                pair = jnp.where(due, p, 0)
+            for p, u in firsts:
+                pair = pair + jnp.where(t == u, p, 0)
+                due = due | (t == u)
+
+            @pl.when(due)
             def _():
-                stage(jnp.where(late, p, 0))
+                stage(pair)
 
     def prepare(t):
-        @pl.when((t >= 1) & (t <= pairs))
-        def _():
-            mm1(t - 1)
+        @pl.loop(0, 2)
+        def _(j):
+            p = 2 * t - 2 + j
+
+            @pl.when((p >= 0) & (p < pairs))
+            def _():
+                mm1(p)
+
+            @pl.when(p == 0)
+            def _():
+                a1(p)
 
     def image_of(k):
         return core + (k % 2) * (1 - 2 * core)
@@ -272,7 +268,7 @@
     start(w_copies)
     start(d_x(0))
     barrier = pltpu.get_barrier_semaphore()
-    neighbours = (dev_ar, dev_al, dev_br, dev_bl, partner)
+    neighbours = (dev_ar, dev_al, dev_br, dev_bl, dev_bo, partner)
     for dev in neighbours:
         pl.semaphore_signal(barrier, inc=1, device_id={"sp": dev}, device_id_type=MESH)
     b1c[...] = jnp.transpose(jnp.broadcast_to(row(bt1_ref), (128, D)))
@@ -286,11 +282,13 @@
 
     @pl.loop(0, FIRST)
     def _(t):
-        slot(t)
-
-        @pl.when(t < pairs)
-        def _():
-            ln1(t)
+        slot(t, lead=True)
+
+        @pl.loop(0, 2)
+        def _(j):
+            @pl.when(2 * t + j < pairs)
+            def _():
+                ln1(2 * t + j)
 
         @pl.when(t == 0)
         def _():
@@ -319,7 +317,7 @@
         mlp(1, None, None, obuf.at[k % 2])
         d_done(k).start()
 
-    @pl.loop(FIRST + 2 * steps, G6[1] + PERIOD * (pairs - 1) + 1)
+    @pl.loop(FIRST + 2 * steps, G6[2] + PERIOD * (pairs - 1) + 1)
     def _(t):
         slot(t)
 
@@ -330,7 +328,7 @@
 
     @pl.loop(0, pairs)
     def _(p):
-        for make in (d_a1, d_a2, d_b1, d_b2, d_g1, d_g2, d_g3, d_g4):
+        for make in (d_a1, d_a2, d_b1, d_g1, d_g3, d_g4):
             for d in make(p):
                 d.wait_send()
         d_g5(p).wait_send()
@@ -340,7 +338,7 @@
         d_out(p).wait()
 
 
-def mlp_half(wt2t, bt2c, s2, o2, w1, c1, w2, c2, v_scr, q_scr, x1_scr, acc, half, x, g, out):
+def mlp_half(wt2t, bt2c, s2, o2, w1, c1, w2, c2, v_scr, q_scr, x1_scr, acc, half, x, g, out, ready=None):
     H, hc = w1.shape[1], q_scr.shape[2]
     steps = H // hc
     if half == 0:
@@ -351,6 +349,8 @@
     for c in range(0, steps // 2) if half == 0 else range(steps // 2, steps + 1):
         if c < steps:
             h = pl.ds(c * hc, hc)
+            if ready is not None:
+                ready(c)
             q_scr[c % 2] = gelu(dot(v_scr[...], w1[:, h]) + row(c1, h)).astype(jnp.bfloat16)
         if c >= 1:
             part = dot(q_scr[(c - 1) % 2], w2[pl.ds((c - 1) * hc, hc), :])
@@ -389,8 +389,7 @@
             pltpu.VMEM((pairs, D, C), f32),
             pltpu.VMEM((pairs, 2, DB, C), f32),
             pltpu.VMEM((pairs, 2, DA, C), f32),
-            pltpu.VMEM((pairs, 2, DB // 2, CB), f32),
-            pltpu.VMEM((pairs, 2, DB, CB), f32),
+            pltpu.VMEM((pairs, 3, DB, CB), f32),
             pltpu.VMEM((pairs, 2, D, C), bf16),
             pltpu.VMEM((D, 2 * S), bf16),
             pltpu.VMEM((D, S), bf16),
@@ -401,8 +400,8 @@
             pltpu.VMEM((2, S, C), bf16),
             pltpu.VMEM((2, S, C), bf16),
             *mlp_scratch(S, C, H),
-            pltpu.SemaphoreType.DMA((18, pairs)),
-            pltpu.SemaphoreType.DMA((18, pairs)),
+            pltpu.SemaphoreType.DMA((16, pairs)),
+            pltpu.SemaphoreType.DMA((16, pairs)),
             pltpu.SemaphoreType.DMA((2, 2)),
             pltpu.SemaphoreType.DMA((5,)),
             pltpu.SemaphoreType.DMA((pairs - done_pairs,)),
@@ -418,34 +417,44 @@
 def finish_kernel(x_hbm, early_hbm, g_hbm, wt2t, bt2c, s2, o2, w1_hbm, c1, w2_hbm, c2, out_hbm,
                   carry, xbuf, gbuf, obuf, w1, w2, v_scr, q_scr, x1_scr, acc, csem, dsem, xsem, gsem, osem, wsem):
     early, rest = carry.shape[0], xbuf.shape[0]
-    w_copies = (pltpu.make_async_copy(w1_hbm, w1, wsem.at[0]), pltpu.make_async_copy(w2_hbm, w2, wsem.at[1]))
+    hc = q_scr.shape[2]
+    ws = []
+    for c in range(w1.shape[1] // hc):
+        h = pl.ds(c * hc, hc)
+        ws.append((pltpu.make_async_copy(w1_hbm.at[:, h], w1.at[:, h], wsem.at[c, 0]),
+                   pltpu.make_async_copy(w2_hbm.at[h, :], w2.at[h, :], wsem.at[c, 1])))
     xs = [pltpu.make_async_copy(x_hbm.at[early + i], xbuf.at[i], xsem.at[i]) for i in range(rest)]
     gs = [pltpu.make_async_copy(g_hbm.at[i // 2, i % 2], gbuf.at[i], gsem.at[i]) for i in range(rest)]
     outs = [pltpu.make_async_copy(obuf.at[i], out_hbm.at[early + i], osem.at[i]) for i in range(rest)]
     ins = [pltpu.make_async_copy(early_hbm.at[i], carry.at[i], csem.at[i]) for i in range(early)]
     backs = [pltpu.make_async_copy(carry.at[i], out_hbm.at[i], dsem.at[i]) for i in range(early)]
-    for i in range(rest):
+    xs[0].start()
+    gs[0].start()
+    for w in ws:
+        w[0].start()
+        w[1].start()
+    for i in range(1, rest):
         xs[i].start()
         gs[i].start()
-        if i == 0:
-            w_copies[0].start()
-            w_copies[1].start()
-    for c in ins:
-        c.start()
+
+    def ready(c):
+        ws[c][0].wait()
+        ws[c][1].wait()
+
     mlp = functools.partial(mlp_half, wt2t, bt2c, s2, o2, w1, c1, w2, c2, v_scr, q_scr, x1_scr, acc)
     for i in range(rest):
         xs[i].wait()
         gs[i].wait()
+        mlp(0, xbuf.at[i], gbuf.at[i], None, ready if i == 0 else None)
         if i == 0:
-            w_copies[0].wait()
-            w_copies[1].wait()
-        mlp(0, xbuf.at[i], gbuf.at[i], None)
+            for c in ins:
+                c.start()
+        mlp(1, None, None, obuf.at[i], ready if i == 0 else None)
+        outs[i].start()
         if i == 0:
             for c, d in zip(ins, backs):
                 c.wait()
                 d.start()
-        mlp(1, None, None, obuf.at[i])
-        outs[i].start()
     for c in (*backs, *outs):
         c.wait()
 
@@ -463,7 +472,7 @@
         out_shape=jax.ShapeDtypeStruct((B, S, C), bf16),
         scratch_shapes=[pltpu.VMEM((n, S, C), bf16), pltpu.VMEM((rest, S, C), bf16), pltpu.VMEM((rest, D, C), bf16),
                         pltpu.VMEM((rest, S, C), bf16), pltpu.VMEM((C, H), bf16), pltpu.VMEM((H, C), bf16),
-                        *mlp_scratch(S, C, H), dma((n,)), dma((n,)), dma((rest,)), dma((rest,)), dma((rest,)), dma((2,))],
+                        *mlp_scratch(S, C, H), dma((n,)), dma((n,)), dma((rest,)), dma((rest,)), dma((rest,)), dma((H // min(512, H // 2), 2))],
         compiler_params=pltpu.CompilerParams(vmem_limit_bytes=60 << 20),
         name="finish",
     )(patches, early, g, wt2t, bt2c, s2, o2, w_ch1, b_ch1, w_ch2, b_ch2)

time: 203 us -> 180 us (0.89)
  Pallas kernels: 202 us -> 180 us
    pallas_call x1, Pallas kernels: 179 us -> 158 us  [exchange(): pl.pallas_call(functools.partial(exchange_kernel, side, done_pairs), out_...]
where the time goes in v3:
time: 180 us
  Pallas kernels  180 us (100%)
    pallas_call x1, Pallas kernels, exchange(): pl.pallas_call(functools.partial(exchange_kernel, side, done_pairs), out_...  158 us
    pallas_call x1, Pallas kernels, finish(): pl.pallas_call(finish_kernel, in_specs=[ANY, ANY, ANY, VMEM, VMEM, VMEM,...  21.1 us

profile of v3, /device:TPU:96, one launch (start us, length us, event | category | flops | bytes accessed | tf_op | source)
XLA Modules:
  0.0 179.7 jit_solution(14724179442068110923)
XLA Ops:
  0.0 158.4 %exchange.1 = (bf16[14,512,768]{2,1,0:T(8,128)(2,1)}, bf16[1,2,384,768]{3,2,1,0:T(8,128)(2,1)}, bf16[512,384]{1,0:T(8,128)(2,1)}, f32[512,128]{1,0:T(8,128)}) custom-call(bf16[16,512,768]{2,1,0:T(8,128)(2,1)} %x_hbm.3, f32[768]{0:T(1024)} %s1_ref.1, f32[768]{0:T(1024)} %o1_ref.1, bf16[16384,384]{1,0:T(8,128)(2,1)} %wt1_hbm.1, f32[384]{0:T(512)} %bt1_ref.1, ...), custom_call_target="tpu_custom_call" | custom-call | tf_op jit(solution)/shard_map/exchange/pallas_call | solution.py:377
  158.4 21.1 %finish.1 = bf16[16,512,768]{2,1,0:T(8,128)(2,1)} custom-call(bf16[16,512,768]{2,1,0:T(8,128)(2,1)} %x_hbm.3, bf16[14,512,768]{2,1,0:T(8,128)(2,1)} %get-tuple-element.9.early_hbm, bf16[1,2,384,768]{3,2,1,0:T(8,128)(2,1)} %get-tuple-element.10.g_hbm, bf16[512,384]{1,0:T(8,128)(2,1)} %get-tuple-element.11.wt2t, f32[512,128]{1,0:T(8,128)} %get-tuple-element.12.bt2c, ...), custom_call_target="tpu_custom_call" | custom-call | tf_op jit(solution)/shard_map/finish/pallas_call | solution.py:468

commit v4 on v3

--- a/solution.py
+++ b/solution.py
@@ -15,9 +15,11 @@
 ANY = pl.BlockSpec(memory_space=pl.ANY)
 VMEM = pl.BlockSpec(memory_space=pltpu.VMEM)
 USLOTS = 4
-FIRST, PERIOD = 7, 4
-A1, A2, B1 = (None, 2, -5), (2, 4, -3), (3, 6, -1)
-G1, G3, G4, G5, G6 = (4, 7, 1), (5, 8, 3), (6, 10, 5), (7, 11, 6), (9, 13, 7)
+FIRST, SHIFT = 8, 2
+PERIOD = 1 << SHIFT
+A1, A2, B1 = (None, None, -6), (2, 3, -4), (3, 5, -1)
+G1, G3, G4, G5, G6 = (4, 6, 1), (5, 8, 3), (6, 9, 5), (7, 11, 7), (9, 13, 9)
+XSLOTS = 4
 
 
 def layer_norm(rows_wide, scale, offset):
@@ -84,7 +86,7 @@
     mine = core
 
     def d_u(p):
-        return remote(0, p, usend.at[p % 2], ubuf.at[p % USLOTS, rows(core * S, S, 16)], partner)
+        return remote(0, p, usend.at[p & 1], ubuf.at[p & (USLOTS - 1), rows(core * S, S, 16)], partner)
 
     def d_a1(p):
         return (remote(1, p, hbuf.at[p, rows(ao * DA, DB, 8)], ra1.at[p, 0], dev_ar),
@@ -115,9 +117,10 @@
         here = gbuf.at[p, mine]
         return remote(15, p, here, here, partner)
 
-    def d_x(p):
-        return (pltpu.make_async_copy(x_hbm.at[2 * p + 1 - core], xbuf.at[p % 2, 0], xsem.at[p % 2, 0]),
-                pltpu.make_async_copy(x_hbm.at[2 * p + core], xbuf.at[p % 2, 1], xsem.at[p % 2, 1]))
+    def d_x(p, own):
+        image = 2 * p + (core if own else 1 - core)
+        n = p & (XSLOTS - 1)
+        return pltpu.make_async_copy(x_hbm.at[image], xbuf.at[n, own], xsem.at[n, own])
 
     def d_out(p):
         return pltpu.make_async_copy(gbuf.at[p], g_out.at[p - done_pairs], osem.at[p - done_pairs])
@@ -138,13 +141,11 @@
 
     LT = min(S, 256)
 
-    def ln1(p):
-        @pl.when(p + 1 < pairs)
-        def _():
-            start(d_x(p + 1))
-
-        other, own = d_x(p)
-        other.wait()
+    def normed(p, which, i):
+        return layer_norm(xbuf[p & (XSLOTS - 1), which, rows(i * LT, LT, LT), :].astype(jnp.float32), row(s1_ref), row(o1_ref))
+
+    def ln_other(p):
+        d_x(p, 0).wait()
 
         @pl.when(p >= 2)
         def _():
@@ -152,25 +153,32 @@
 
         @pl.loop(0, S // LT)
         def _(i):
-            r = rows(i * LT, LT, LT)
-            usend[p % 2, r, :] = layer_norm(xbuf[p % 2, 0, r, :].astype(jnp.float32), row(s1_ref), row(o1_ref))
-
-        @pl.when(p >= USLOTS)
-        def _():
-            pl.semaphore_wait(credit, 1)
-
-        d_u(p).start()
-        own.wait()
+            usend[p & 1, rows(i * LT, LT, LT), :] = normed(p, 0, i)
+
+    def ln1(p):
+        @pl.when(p + XSLOTS - 1 < pairs)
+        def _():
+            start((d_x(p + XSLOTS - 1, 0), d_x(p + XSLOTS - 1, 1)))
+
+        @pl.when(p > 0)
+        def _():
+            ln_other(p)
+
+            @pl.when(p >= USLOTS)
+            def _():
+                pl.semaphore_wait(credit, 1)
+
+            d_u(p).start()
+
+        d_x(p, 1).wait()
 
         @pl.loop(0, S // LT)
         def _(i):
-            r = rows(i * LT, LT, LT)
-            ubuf[p % USLOTS, rows(core * S + i * LT, LT, LT), :] = layer_norm(
-                xbuf[p % 2, 1, r, :].astype(jnp.float32), row(s1_ref), row(o1_ref))
+            ubuf[p & (USLOTS - 1), rows(core * S + i * LT, LT, LT), :] = normed(p, 1, i)
 
     def mm1(p):
         d_u(p).wait_recv()
-        hbuf[p] = dot(wt1t[...], ubuf[p % USLOTS])
+        hbuf[p] = dot(wt1t[...], ubuf[p & (USLOTS - 1)])
 
         @pl.when(p + USLOTS < pairs)
         def _():
@@ -219,10 +227,10 @@
     plan = ((g6, G6), (g5, G5), (g4, G4), (g3, G3), (g1, G1), (b1, B1), (a2, A2), (a1, A1))
 
     def slot(t, parity=None, lead=False):
-        for stage, (first, second, later) in plan:
+        for stage, (*fixed, later) in plan:
             if lead and stage is a1:
                 prepare(t)
-            firsts = [(p, u) for p, u in enumerate((first, second))
+            firsts = [(p, u) for p, u in enumerate(fixed)
                       if u is not None and (lead == (u < FIRST)) and (lead or parity is None or (u - parity) % 2 == 0)]
             even = parity is None or (later - parity) % 2 == 0
             if not even and not firsts:
@@ -230,8 +238,8 @@
             due, pair = False, 0
             if even:
                 q = t + PERIOD * pairs - later
-                p = q // PERIOD - pairs
-                due = (q % PERIOD == 0) & (p >= 2) & (p < pairs)
+                p = (q >> SHIFT) - pairs
+                due = (q & (PERIOD - 1) == 0) & (p >= len(fixed)) & (p < pairs)
                 pair = jnp.where(due, p, 0)
             for p, u in firsts:
                 pair = pair + jnp.where(t == u, p, 0)
@@ -241,54 +249,59 @@
             def _():
                 stage(pair)
 
+    def upto(t):
+        return 2 + ((3 * t) >> 1)
+
     def prepare(t):
-        @pl.loop(0, 2)
-        def _(j):
-            p = 2 * t - 2 + j
-
+        @pl.loop(upto(t - 2), upto(t - 1))
+        def _(p):
             @pl.when((p >= 0) & (p < pairs))
             def _():
                 mm1(p)
 
-            @pl.when(p == 0)
-            def _():
-                a1(p)
+                @pl.when(p < 2)
+                def _():
+                    a1(p)
 
     def image_of(k):
-        return core + (k % 2) * (1 - 2 * core)
+        return core + (k & 1) * (1 - 2 * core)
 
     def d_res(k):
-        return pltpu.make_async_copy(x_hbm.at[(k // 2) * 2 + image_of(k)], xres.at[k % 2], xrsem.at[k % 2])
+        return pltpu.make_async_copy(x_hbm.at[(k >> 1) * 2 + image_of(k)], xres.at[k & 1], xrsem.at[k & 1])
 
     def d_done(k):
-        return pltpu.make_async_copy(obuf.at[k % 2], out_hbm.at[(k // 2) * 2 + image_of(k)], obsem.at[k % 2])
-
-    mlp = functools.partial(mlp_half, wt2t_ref, bt2c_ref, s2_ref, o2_ref, w1, c1_ref, w2, c2_ref, v_scr, q_scr, x1_scr, acc)
-
-    start(w_copies)
-    start(d_x(0))
+        return pltpu.make_async_copy(obuf.at[k & 1], out_hbm.at[(k >> 1) * 2 + image_of(k)], obsem.at[k & 1])
+
+    pre, mlp = channel_mlp(wt2t_ref, bt2c_ref, s2_ref, o2_ref, w1, c1_ref, w2, c2_ref, v_scr, q_scr, x1_scr, acc)
+    steps = 2 * done_pairs
+
+    start((d_x(0, 0), d_x(0, 1)))
     barrier = pltpu.get_barrier_semaphore()
     neighbours = (dev_ar, dev_al, dev_br, dev_bl, dev_bo, partner)
     for dev in neighbours:
         pl.semaphore_signal(barrier, inc=1, device_id={"sp": dev}, device_id_type=MESH)
+    start(w_copies)
+    for p in range(1, XSLOTS - 1):
+        start((d_x(p, 0), d_x(p, 1)))
+    ln_other(0)
+    pl.semaphore_wait(barrier, len(neighbours))
+    d_u(0).start()
     b1c[...] = jnp.transpose(jnp.broadcast_to(row(bt1_ref), (128, D)))
     for w in w_copies:
         w.wait()
+    wt1t[...] = jnp.transpose(wt1[...])
     start(ch_copies)
     d_res(0).start()
-    wt1t[...] = jnp.transpose(wt1[...])
-    pl.semaphore_wait(barrier, len(neighbours))
-    steps = 2 * done_pairs
 
     @pl.loop(0, FIRST)
     def _(t):
         slot(t, lead=True)
 
-        @pl.loop(0, 2)
-        def _(j):
-            @pl.when(2 * t + j < pairs)
+        @pl.loop(upto(t - 1), upto(t))
+        def _(p):
+            @pl.when(p < pairs)
             def _():
-                ln1(2 * t + j)
+                ln1(p)
 
         @pl.when(t == 0)
         def _():
@@ -297,6 +310,8 @@
 
     for w in ch_copies:
         w.wait()
+    d_res(0).wait()
+    pre(0, xres.at[0], gbuf.at[0, image_of(0)])
 
     @pl.loop(0, steps)
     def _(k):
@@ -306,18 +321,23 @@
         def _():
             d_res(k + 1).start()
 
-        d_res(k).wait()
-        mlp(0, xres.at[k % 2], gbuf.at[k // 2, image_of(k)], None)
+        mlp(0, k & 1)
         slot(FIRST + 2 * k + 1, (FIRST + 1) % 2)
 
+        @pl.when(k + 1 < steps)
+        def _():
+            d_res(k + 1).wait()
+
         @pl.when(k >= 2)
         def _():
             d_done(k - 2).wait()
 
-        mlp(1, None, None, obuf.at[k % 2])
+        following = jnp.minimum(k + 1, steps - 1)
+        mlp(1, k & 1, obuf.at[k & 1],
+            lambda: pre((k + 1) & 1, xres.at[(k + 1) & 1], gbuf.at[following >> 1, image_of(following)]))
         d_done(k).start()
 
-    @pl.loop(FIRST + 2 * steps, G6[2] + PERIOD * (pairs - 1) + 1)
+    @pl.loop(FIRST + 2 * steps, G6[-1] + PERIOD * (pairs - 1) + 1)
     def _(t):
         slot(t)
 
@@ -338,34 +358,41 @@
         d_out(p).wait()
 
 
-def mlp_half(wt2t, bt2c, s2, o2, w1, c1, w2, c2, v_scr, q_scr, x1_scr, acc, half, x, g, out, ready=None):
+def channel_mlp(wt2t, bt2c, s2, o2, w1, c1, w2, c2, v_scr, q_scr, x1_scr, acc):
     H, hc = w1.shape[1], q_scr.shape[2]
     steps = H // hc
-    if half == 0:
+
+    def pre(i, x, g):
         t = (dot(wt2t[...], g[...]) + bt2c[:, 0:1]).astype(jnp.bfloat16)
         x1 = (x[...].astype(jnp.float32) + t.astype(jnp.float32)).astype(jnp.bfloat16)
-        x1_scr[...] = x1
-        v_scr[...] = layer_norm(x1.astype(jnp.float32), row(s2), row(o2))
-    for c in range(0, steps // 2) if half == 0 else range(steps // 2, steps + 1):
-        if c < steps:
-            h = pl.ds(c * hc, hc)
-            if ready is not None:
-                ready(c)
-            q_scr[c % 2] = gelu(dot(v_scr[...], w1[:, h]) + row(c1, h)).astype(jnp.bfloat16)
-        if c >= 1:
-            part = dot(q_scr[(c - 1) % 2], w2[pl.ds((c - 1) * hc, hc), :])
-            if c == 1:
-                acc[...] = part + row(c2)
-            elif c < steps:
-                acc[...] += part
-            else:
-                out[...] = (x1_scr[...].astype(jnp.float32) + (acc[...] + part)).astype(jnp.bfloat16)
+        x1_scr[i] = x1
+        v_scr[i] = layer_norm(x1.astype(jnp.float32), row(s2), row(o2))
+
+    def half(which, i, out=None, beside=None, ready=None):
+        for c in range(0, steps // 2) if which == 0 else range(steps // 2, steps + 1):
+            if c < steps:
+                h = pl.ds(c * hc, hc)
+                if ready is not None:
+                    ready(c)
+                q_scr[c % 2] = gelu(dot(v_scr[i], w1[:, h]) + row(c1, h)).astype(jnp.bfloat16)
+            if c >= 1:
+                part = dot(q_scr[(c - 1) % 2], w2[pl.ds((c - 1) * hc, hc), :])
+                if c == 1:
+                    acc[...] = part + row(c2)
+                elif c < steps:
+                    acc[...] += part
+                else:
+                    out[...] = (x1_scr[i].astype(jnp.float32) + (acc[...] + part)).astype(jnp.bfloat16)
+            if c == steps - 1 and beside is not None:
+                beside()
+
+    return pre, half
 
 
 def mlp_scratch(S, C, H):
-    hc = min(512, H // 2)
-    return [pltpu.VMEM((S, C), jnp.bfloat16), pltpu.VMEM((2, S, hc), jnp.bfloat16),
-            pltpu.VMEM((S, C), jnp.bfloat16), pltpu.VMEM((S, C), jnp.float32)]
+    hc = H // 4
+    return [pltpu.VMEM((2, S, C), jnp.bfloat16), pltpu.VMEM((2, S, hc), jnp.bfloat16),
+            pltpu.VMEM((2, S, C), jnp.bfloat16), pltpu.VMEM((S, C), jnp.float32)]
 
 
 def exchange(side, done_pairs, patches, s1, o1, w_tok1, b_tok1, w_tok2, b_tok2, s2, o2, w_ch1, b_ch1, w_ch2, b_ch2):
@@ -383,7 +410,7 @@
         in_specs=[ANY, VMEM, VMEM, ANY, VMEM, ANY, ANY, VMEM, VMEM, ANY, VMEM, ANY, VMEM],
         out_specs=(ANY, ANY, VMEM, VMEM),
         scratch_shapes=[
-            pltpu.VMEM((2, 2, S, C), bf16),
+            pltpu.VMEM((XSLOTS, 2, S, C), bf16),
             pltpu.VMEM((2, S, C), bf16),
             pltpu.VMEM((USLOTS, 2 * S, C), bf16),
             pltpu.VMEM((pairs, D, C), f32),
@@ -402,7 +429,7 @@
             *mlp_scratch(S, C, H),
             pltpu.SemaphoreType.DMA((16, pairs)),
             pltpu.SemaphoreType.DMA((16, pairs)),
-            pltpu.SemaphoreType.DMA((2, 2)),
+            pltpu.SemaphoreType.DMA((XSLOTS, 2)),
             pltpu.SemaphoreType.DMA((5,)),
             pltpu.SemaphoreType.DMA((pairs - done_pairs,)),
             pltpu.SemaphoreType.DMA((2,)),
@@ -414,8 +441,8 @@
     )(patches, s1, o1, w_tok1, b_tok1, w_tok2, b_tok2, s2, o2, w_ch1, b_ch1, w_ch2, b_ch2)
 
 
-def finish_kernel(x_hbm, early_hbm, g_hbm, wt2t, bt2c, s2, o2, w1_hbm, c1, w2_hbm, c2, out_hbm,
-                  carry, xbuf, gbuf, obuf, w1, w2, v_scr, q_scr, x1_scr, acc, csem, dsem, xsem, gsem, osem, wsem):
+def finish_kernel(x_hbm, early_hbm, g_hbm, wt2t_hbm, bt2c_hbm, s2, o2, w1_hbm, c1, w2_hbm, c2, out_hbm,
+                  carry, xbuf, gbuf, obuf, wt2t, bt2c, w1, w2, v_scr, q_scr, x1_scr, acc, csem, dsem, xsem, gsem, osem, wsem, tsem):
     early, rest = carry.shape[0], xbuf.shape[0]
     hc = q_scr.shape[2]
     ws = []
@@ -428,8 +455,10 @@
     outs = [pltpu.make_async_copy(obuf.at[i], out_hbm.at[early + i], osem.at[i]) for i in range(rest)]
     ins = [pltpu.make_async_copy(early_hbm.at[i], carry.at[i], csem.at[i]) for i in range(early)]
     backs = [pltpu.make_async_copy(carry.at[i], out_hbm.at[i], dsem.at[i]) for i in range(early)]
-    xs[0].start()
-    gs[0].start()
+    ts = (pltpu.make_async_copy(wt2t_hbm, wt2t, tsem.at[0]), pltpu.make_async_copy(bt2c_hbm, bt2c, tsem.at[1]))
+    first = (*ts, xs[0], gs[0])
+    for c in first:
+        c.start()
     for w in ws:
         w[0].start()
         w[1].start()
@@ -441,15 +470,22 @@
         ws[c][0].wait()
         ws[c][1].wait()
 
-    mlp = functools.partial(mlp_half, wt2t, bt2c, s2, o2, w1, c1, w2, c2, v_scr, q_scr, x1_scr, acc)
+    def following(i):
+        return lambda: pre(i & 1, xbuf.at[i], gbuf.at[i]) if i < rest else None
+
+    pre, mlp = channel_mlp(wt2t, bt2c, s2, o2, w1, c1, w2, c2, v_scr, q_scr, x1_scr, acc)
+    for c in first:
+        c.wait()
+    pre(0, xbuf.at[0], gbuf.at[0])
     for i in range(rest):
-        xs[i].wait()
-        gs[i].wait()
-        mlp(0, xbuf.at[i], gbuf.at[i], None, ready if i == 0 else None)
+        mlp(0, i & 1, ready=ready if i == 0 else None)
         if i == 0:
             for c in ins:
                 c.start()
-        mlp(1, None, None, obuf.at[i], ready if i == 0 else None)
+        if i + 1 < rest:
+            xs[i + 1].wait()
+            gs[i + 1].wait()
+        mlp(1, i & 1, obuf.at[i], following(i + 1), ready if i == 0 else None)
         outs[i].start()
         if i == 0:
             for c, d in zip(ins, backs):
@@ -467,12 +503,13 @@
     dma = pltpu.SemaphoreType.DMA
     return pl.pallas_call(
         finish_kernel,
-        in_specs=[ANY, ANY, ANY, VMEM, VMEM, VMEM, VMEM, ANY, VMEM, ANY, VMEM],
+        in_specs=[ANY, ANY, ANY, ANY, ANY, VMEM, VMEM, ANY, VMEM, ANY, VMEM],
         out_specs=ANY,
         out_shape=jax.ShapeDtypeStruct((B, S, C), bf16),
         scratch_shapes=[pltpu.VMEM((n, S, C), bf16), pltpu.VMEM((rest, S, C), bf16), pltpu.VMEM((rest, D, C), bf16),
-                        pltpu.VMEM((rest, S, C), bf16), pltpu.VMEM((C, H), bf16), pltpu.VMEM((H, C), bf16),
-                        *mlp_scratch(S, C, H), dma((n,)), dma((n,)), dma((rest,)), dma((rest,)), dma((rest,)), dma((H // min(512, H // 2), 2))],
+                        pltpu.VMEM((rest, S, C), bf16), pltpu.VMEM((S, D), bf16), pltpu.VMEM((S, 128), jnp.float32),
+                        pltpu.VMEM((C, H), bf16), pltpu.VMEM((H, C), bf16),
+                        *mlp_scratch(S, C, H), dma((n,)), dma((n,)), dma((rest,)), dma((rest,)), dma((rest,)), dma((4, 2)), dma((2,))],
         compiler_params=pltpu.CompilerParams(vmem_limit_bytes=60 << 20),
         name="finish",
     )(patches, early, g, wt2t, bt2c, s2, o2, w_ch1, b_ch1, w_ch2, b_ch2)

time: 180 us -> 167 us (0.928)
  Pallas kernels: 180 us -> 167 us
    pallas_call x1, Pallas kernels: 158 us -> 147 us  [exchange(): pl.pallas_call(functools.partial(exchange_kernel, side, done_pairs), out_...]
where the time goes in v4:
time: 167 us
  Pallas kernels  167 us (100%)
    pallas_call x1, Pallas kernels, exchange(): pl.pallas_call(functools.partial(exchange_kernel, side, done_pairs), out_...  147 us
    pallas_call x1, Pallas kernels, finish(): pl.pallas_call(finish_kernel, in_specs=[ANY, ANY, ANY, ANY, ANY, VMEM, VM...  19.5 us

profile of v4, /device:TPU:96, one launch (start us, length us, event | category | flops | bytes accessed | tf_op | source)
XLA Modules:
  0.0 166.7 jit_solution(18376875907707077898)
XLA Ops:
  0.0 147.0 %exchange.1 = (bf16[14,512,768]{2,1,0:T(8,128)(2,1)}, bf16[1,2,384,768]{3,2,1,0:T(8,128)(2,1)}, bf16[512,384]{1,0:T(8,128)(2,1)}, f32[512,128]{1,0:T(8,128)}) custom-call(bf16[16,512,768]{2,1,0:T(8,128)(2,1)} %x_hbm.3, f32[768]{0:T(1024)} %s1_ref.1, f32[768]{0:T(1024)} %o1_ref.1, bf16[16384,384]{1,0:T(8,128)(2,1)} %wt1_hbm.1, f32[384]{0:T(512)} %bt1_ref.1, ...), custom_call_target="tpu_custom_call" | custom-call | tf_op jit(solution)/shard_map/exchange/pallas_call | solution.py:404
  147.0 19.5 %finish.1 = bf16[16,512,768]{2,1,0:T(8,128)(2,1)} custom-call(bf16[16,512,768]{2,1,0:T(8,128)(2,1)} %x_hbm.3, bf16[14,512,768]{2,1,0:T(8,128)(2,1)} %get-tuple-element.9.early_hbm, bf16[1,2,384,768]{3,2,1,0:T(8,128)(2,1)} %get-tuple-element.10.g_hbm, bf16[512,384]{1,0:T(8,128)(2,1)} %get-tuple-element.11.wt2t_hbm, f32[512,128]{1,0:T(8,128)} %get-tuple-element.12.bt2c_hbm, ...), custom_call_target="tpu_custom_call" | custom-call | tf_op jit(solution)/shard_map/finish/pallas_call | solution.py:504

commit v5 on v4

--- a/solution.py
+++ b/solution.py
@@ -48,9 +48,9 @@
 
 def exchange_kernel(side, done_pairs, x_hbm, s1_ref, o1_ref, wt1_hbm, bt1_ref, wt2_hbm, bt2_hbm,
                     s2_ref, o2_ref, w1_hbm, c1_ref, w2_hbm, c2_ref,
-                    out_hbm, g_out, wt2t_ref, bt2c_ref,
+                    out_hbm, g_out, wt2t_out, bt2c_out,
                     xbuf, usend, ubuf, hbuf, ra1, ra2, rb, gbuf, wt1t, wt2, bt2, b1c,
-                    w1, w2, xres, obuf, v_scr, q_scr, x1_scr, acc,
+                    w1, w2, wt2t_ref, bt2c_ref, xres, obuf, v_scr, q_scr, x1_scr, acc,
                     ssem, rsem, xsem, wsem, osem, xrsem, obsem, credit):
     B, S, C = x_hbm.shape
     pairs = B // 2
@@ -126,6 +126,7 @@
         return pltpu.make_async_copy(gbuf.at[p], g_out.at[p - done_pairs], osem.at[p - done_pairs])
 
     wt1 = ubuf.at[USLOTS - 1, :, pl.ds(0, D)] if D <= C else None
+    t_copies = (pltpu.make_async_copy(wt2t_ref, wt2t_out, wsem.at[5]), pltpu.make_async_copy(bt2c_ref, bt2c_out, wsem.at[6]))
     ch_copies = (pltpu.make_async_copy(w1_hbm, w1, wsem.at[3]), pltpu.make_async_copy(w2_hbm, w2, wsem.at[4]))
     w_copies = (pltpu.make_async_copy(wt1_hbm.at[rows(chip * 2 * S, 2 * S, 16)], wt1, wsem.at[0]),
                 pltpu.make_async_copy(wt2_hbm.at[:, rows(me * S, S, 128)], wt2, wsem.at[1]),
@@ -308,6 +309,7 @@
             wt2t_ref[...] = jnp.transpose(wt2[...])
             bt2c_ref[...] = jnp.transpose(jnp.broadcast_to(bt2[...], (128, S)))
 
+    start(t_copies)
     for w in ch_copies:
         w.wait()
     d_res(0).wait()
@@ -343,6 +345,8 @@
 
     d_done(steps - 2).wait()
     d_done(steps - 1).wait()
+    for w in t_copies:
+        w.wait()
     for p in (pairs - 2, pairs - 1):
         d_u(p).wait_send()
 
@@ -408,7 +412,7 @@
                    jax.ShapeDtypeStruct((S, D), bf16),
                    jax.ShapeDtypeStruct((S, 128), f32)),
         in_specs=[ANY, VMEM, VMEM, ANY, VMEM, ANY, ANY, VMEM, VMEM, ANY, VMEM, ANY, VMEM],
-        out_specs=(ANY, ANY, VMEM, VMEM),
+        out_specs=(ANY, ANY, ANY, ANY),
         scratch_shapes=[
             pltpu.VMEM((XSLOTS, 2, S, C), bf16),
             pltpu.VMEM((2, S, C), bf16),
@@ -424,13 +428,15 @@
             pltpu.VMEM((D, 128), f32),
             pltpu.VMEM((C, H), bf16),
             pltpu.VMEM((H, C), bf16),
+            pltpu.VMEM((S, D), bf16),
+            pltpu.VMEM((S, 128), f32),
             pltpu.VMEM((2, S, C), bf16),
             pltpu.VMEM((2, S, C), bf16),
             *mlp_scratch(S, C, H),
             pltpu.SemaphoreType.DMA((16, pairs)),
             pltpu.SemaphoreType.DMA((16, pairs)),
             pltpu.SemaphoreType.DMA((XSLOTS, 2)),
-            pltpu.SemaphoreType.DMA((5,)),
+            pltpu.SemaphoreType.DMA((7,)),
             pltpu.SemaphoreType.DMA((pairs - done_pairs,)),
             pltpu.SemaphoreType.DMA((2,)),
             pltpu.SemaphoreType.DMA((2,)),

time: 167 us -> 166 us (level)
  no operation moved by 1% of the time
where the time goes in v5:
time: 166 us
  Pallas kernels  166 us (100%)
    pallas_call x1, Pallas kernels, exchange(): pl.pallas_call(functools.partial(exchange_kernel, side, done_pairs), out_...  146 us
    pallas_call x1, Pallas kernels, finish(): pl.pallas_call(finish_kernel, in_specs=[ANY, ANY, ANY, ANY, ANY, VMEM, VM...  19.5 us

profile of v5, /device:TPU:96, one launch (start us, length us, event | category | flops | bytes accessed | tf_op | source)
XLA Modules:
  0.0 165.9 jit_solution(9976817583892614461)
XLA Ops:
  0.0 146.2 %exchange.1 = (bf16[14,512,768]{2,1,0:T(8,128)(2,1)}, bf16[1,2,384,768]{3,2,1,0:T(8,128)(2,1)}, bf16[512,384]{1,0:T(8,128)(2,1)}, f32[512,128]{1,0:T(8,128)}) custom-call(bf16[16,512,768]{2,1,0:T(8,128)(2,1)} %x_hbm.3, f32[768]{0:T(1024)} %s1_ref.1, f32[768]{0:T(1024)} %o1_ref.1, bf16[16384,384]{1,0:T(8,128)(2,1)} %wt1_hbm.1, f32[384]{0:T(512)} %bt1_ref.1, ...), custom_call_target="tpu_custom_call" | custom-call | tf_op jit(solution)/shard_map/exchange/pallas_call | solution.py:408
  146.2 19.5 %finish.1 = bf16[16,512,768]{2,1,0:T(8,128)(2,1)} custom-call(bf16[16,512,768]{2,1,0:T(8,128)(2,1)} %x_hbm.3, bf16[14,512,768]{2,1,0:T(8,128)(2,1)} %get-tuple-element.9.early_hbm, bf16[1,2,384,768]{3,2,1,0:T(8,128)(2,1)} %get-tuple-element.10.g_hbm, bf16[512,384]{1,0:T(8,128)(2,1)} %get-tuple-element.11.wt2t_hbm, f32[512,128]{1,0:T(8,128)} %get-tuple-element.12.bt2c_hbm, ...), custom_call_target="tpu_custom_call" | custom-call | tf_op jit(solution)/shard_map/finish/pallas_call | solution.py:510
